TPU v7x, 32 devices: a whole 2x2x4 slice. The times are simulated.
32 devices in a mesh: batch: 2 (over x), col: 4 (over z), row: 4 (over y, core).
Axes of the slice: x: 2, y: 2, z: 4, core: 2. Of those that a mesh axis runs over, the one named last changes fastest.
Arguments:
- x: bfloat16 [32, 1024, 32, 64], P('batch', 'row', 'col'), parts along dimension 0
- w_down_1: bfloat16 [3, 3, 64, 128], replicated
- b_down_1: float32 [128], replicated
- w_conv_1: bfloat16 [3, 3, 128, 128], replicated
- b_conv_1: float32 [128], replicated
- w_proj_1: bfloat16 [64, 128], replicated
- w_down_2: bfloat16 [3, 3, 128, 256], replicated
- b_down_2: float32 [256], replicated
- w_conv_2: bfloat16 [3, 3, 256, 256], replicated
- b_conv_2: float32 [256], replicated
- w_proj_2: bfloat16 [128, 256], replicated
- w_down_3: bfloat16 [3, 3, 256, 320], replicated
- b_down_3: float32 [320], replicated
- w_conv_3: bfloat16 [3, 3, 320, 320], replicated
- b_conv_3: float32 [320], replicated
- w_proj_3: bfloat16 [256, 320], replicated
Outputs:
- output: bfloat16 [32, 128, 4, 320], P('batch', 'row', 'col'), parts along dimension 0
There are 2 independent parts. A program takes and returns all parts, laid end to end along the dimension named above; an argument that names none is the same for every part.
All inputs are finite; a program needn't handle non-finite values.
Results may differ from a plain program's by a relative error of at most 0.00368202.
Values are sent between devices in bfloat16 or wider.
A program may use at most 1 GiB of HBM per device.

v0:
```python
import jax
import jax.numpy as jnp
from jax import lax
from jax.sharding import PartitionSpec as P

CONV_DIMS = ("NHWC", "HWIO", "NHWC")


def from_lower(edge_part, axis_name, dev_count):
    return lax.ppermute(edge_part, axis_name, [(dev_index, dev_index + 1) for dev_index in range(dev_count - 1)])


def from_upper(edge_part, axis_name, dev_count):
    return lax.ppermute(edge_part, axis_name, [(dev_index + 1, dev_index) for dev_index in range(dev_count - 1)])


def pad_lower(tile_in, row_count, col_count):
    top_row = from_lower(tile_in[:, -1:], "row", row_count)
    tall_tile = jnp.concatenate([top_row, tile_in], axis=1)
    left_col = from_lower(tall_tile[:, :, -1:], "col", col_count)
    return jnp.concatenate([left_col, tall_tile], axis=2)


def pad_both(tile_in, row_count, col_count):
    top_row = from_lower(tile_in[:, -1:], "row", row_count)
    bottom_row = from_upper(tile_in[:, :1], "row", row_count)
    tall_tile = jnp.concatenate([top_row, tile_in, bottom_row], axis=1)
    left_col = from_lower(tall_tile[:, :, -1:], "col", col_count)
    right_col = from_upper(tall_tile[:, :, :1], "col", col_count)
    return jnp.concatenate([left_col, tall_tile, right_col], axis=2)


def conv_valid(act_in, weight, stride):
    return lax.conv_general_dilated(act_in, weight, (stride, stride), "VALID", dimension_numbers=CONV_DIMS, preferred_element_type=jnp.float32)


def basic_block(z_prev, w_down, b_down, w_conv, b_conv, w_proj, row_count, col_count):
    y_act = jax.nn.relu(conv_valid(pad_lower(z_prev, row_count, col_count), w_down, 2) + b_down).astype(jnp.bfloat16)
    shortcut = jnp.einsum("bhwc,cd->bhwd", z_prev[:, ::2, ::2], w_proj, preferred_element_type=jnp.float32)
    z_next = jax.nn.relu(conv_valid(pad_both(y_act, row_count, col_count), w_conv, 1) + shortcut + b_conv)
    return z_next.astype(jnp.bfloat16)


def solution(mesh):
    row_count = mesh.shape["row"]
    col_count = mesh.shape["col"]
    tile_spec = P("batch", "row", "col")

    def local_blocks(x_tile, *params):
        act_out = x_tile
        for stage in range(3):
            stage_params = params[5 * stage:5 * stage + 5]
            act_out = basic_block(act_out, stage_params[0], stage_params[1], stage_params[2], stage_params[3], stage_params[4], row_count, col_count)
        return act_out

    return jax.shard_map(local_blocks, mesh=mesh, in_specs=(tile_spec,) + (P(),) * 15, out_specs=tile_spec, check_vma=False)
```

profile of v0, /device:TPU:1, one launch (start us, length us, event | category | flops | bytes accessed | tf_op | source)
XLA Modules:
  0.0 222.2 jit_solution(7310056246200079597)
XLA Ops:
  0.0 13.2 %copy.25 = bf16[16,256,8,64]{3,0,2,1:T(8,128)(2,1)} copy(bf16[16,256,8,64]{1,3,2,0:T(8,128)(2,1)} %param.16) | data formatting | bytes 8388608 | tf_op args[0]
  13.2 0.8 slice.77
  13.9 4.5 %collective-permute-start = (bf16[16,1,8,64]{3,0,2,1:T(8,128)(2,1)S(1)}, bf16[16,1,8,64]{3,0,2,1:T(8,128)(2,1)S(1)}, u32[]{:S(2)}, u32[]{:S(2)}) collective-permute-start(bf16[16,1,8,64]{3,0,2,1:T(8,128)(2,1)S(1)} %slice.77), channel_id=1, source_target_pairs={{0,1},{1,2},{2,3},{4,5},{5,6},{6,7},{8,9},{9,10},{10,11},{12,13},{... | collective-permute-start | bytes 49160 | tf_op jit(solution)/shard_map/ppermute | solution.py:10
  18.5 1.0 collective-permute-done
  19.5 1.5 pad_maximum_fusion.1
  21.0 1.6 copy.27
  22.6 4.1 %collective-permute-start.1 = (bf16[16,257,1,64]{1,3,2,0:T(8,128)(2,1)}, bf16[16,257,1,64]{1,3,2,0:T(8,128)(2,1)}, u32[]{:S(2)}, u32[]{:S(2)}) collective-permute-start(bf16[16,257,1,64]{1,3,2,0:T(8,128)(2,1)} %copy.27), channel_id=1, source_target_pairs={{0,4},{4,8},{8,12},{1,5},{5,9},{9,13},{2,6},{6,10},{10,14},{3,7},{... | collective-permute-start | bytes 1579016 | tf_op jit(solution)/shard_map/ppermute | solution.py:10
  26.7 15.5 %collective-permute-done.1 = bf16[16,257,1,64]{1,3,2,0:T(8,128)(2,1)} collective-permute-done((bf16[16,257,1,64]{1,3,2,0:T(8,128)(2,1)}, bf16[16,257,1,64]{1,3,2,0:T(8,128)(2,1)}, u32[]{:S(2)}, u32[]{:S(2)}) %collective-permute-start.1) | collective-permute-done | bytes 526368 | tf_op jit(solution)/shard_map/ppermute | solution.py:10
  42.1 1.9 copy.28
  44.1 7.0 %maximum_convert_fusion.1 = bf16[16,128,4,128]{3,0,2,1:T(8,128)(2,1)S(1)} fusion(f32[128]{0:T(128)S(1)} %copy-done.15, bf16[3,3,64,128]{3,2,1,0:T(8,128)(2,1)S(1)} %copy-done.10, bf16[16,256,8,64]{3,0,2,1:T(8,128)(2,1)} %copy.25, bf16[16,1,8,64]{3,0,2,1:T(8,128)(2,1)S(1)} %collective-permute-done, bf16[16,257,1,64]{3,0,2,1:T(8,128)(2,1)S(1)} %copy.28), kind=kOutput, calls=%fused_computation.7 | convolution fusion | flops 1215842304 | bytes 6982144 | tf_op jit(solution)/shard_map/conv_general_dilated | solution.py:34
  51.1 3.0 %collective-permute-start.2 = (bf16[16,1,4,128]{3,0,2,1:T(8,128)(2,1)S(1)}, bf16[16,1,4,128]{3,0,2,1:T(8,128)(2,1)S(1)}, u32[]{:S(2)}, u32[]{:S(2)}) collective-permute-start(bf16[16,1,4,128]{3,0,2,1:T(8,128)(2,1)S(1)} %get-tuple-element.7), channel_id=1, source_target_pairs={{0,1},{1,2},{2,3},{4,5},{5,6},{6,7},{8,9},{9,10},{10,11},{12,13},{... | collective-permute-start | bytes 49160 | tf_op jit(solution)/shard_map/ppermute | solution.py:10
  54.1 1.9 collective-permute-start.3
  56.0 3.1 %collective-permute-done.3 = bf16[16,1,4,128]{3,0,2,1:T(8,128)(2,1)S(1)} collective-permute-done((bf16[16,1,4,128]{3,0,2,1:T(8,128)(2,1)S(1)}, bf16[16,1,4,128]{3,0,2,1:T(8,128)(2,1)S(1)}, u32[]{:S(2)}, u32[]{:S(2)}) %collective-permute-start.3) | collective-permute-done | bytes 16416 | tf_op jit(solution)/shard_map/ppermute | solution.py:14
  59.1 1.2 pad_maximum_fusion.5
  60.3 5.0 %collective-permute-start.4 = (bf16[16,130,1,128]{3,0,2,1:T(8,128)(2,1)}, bf16[16,130,1,128]{3,0,2,1:T(8,128)(2,1)}, u32[]{:S(2)}, u32[]{:S(2)}) collective-permute-start(bf16[16,130,1,128]{3,0,2,1:T(8,128)(2,1)} %get-tuple-element.5), channel_id=1, source_target_pairs={{0,4},{4,8},{8,12},{1,5},{5,9},{9,13},{2,6},{6,10},{10,14},{3,7},{... | collective-permute-start | bytes 1597448 | tf_op jit(solution)/shard_map/ppermute | solution.py:10
  65.2 1.3 collective-permute-start.5
  66.5 47.6 %slice.64 = bf16[16,128,4,64]{1,3,2,0:T(8,128)(2,1)S(1)} slice(bf16[16,256,8,64]{1,3,2,0:T(8,128)(2,1)} %param.16), slice={[0:16:1], [0:256:2], [0:8:2], [0:64:1]} | slice | bytes 2097152 | tf_op jit(solution)/shard_map/slice | solution.py:39
  114.1 3.7 %copy.35 = bf16[16,128,4,64]{3,0,2,1:T(8,128)(2,1)} copy(bf16[16,128,4,64]{1,3,2,0:T(8,128)(2,1)S(1)} %slice.64) | data formatting | bytes 2097152 | tf_op jit(solution)/shard_map/slice | solution.py:39
  117.8 2.4 %fusion.75 = f32[16,128,4,128]{3,0,2,1:T(8,128)S(1)} fusion(bf16[16,128,4,64]{3,0,2,1:T(8,128)(2,1)} %copy.35, bf16[64,128]{1,0:T(8,128)(2,1)S(1)} %copy-done.5), kind=kOutput, calls=%fused_computation.73 | convolution fusion | flops 134217728 | bytes 5259264 | tf_op jit(solution)/shard_map/bhwc,cd->bhwd/dot_general | solution.py:39
  120.3 6.5 %maximum_convert_fusion = bf16[16,128,4,128]{3,0,2,1:T(8,128)(2,1)S(1)} fusion(f32[16,128,4,128]{3,0,2,1:T(8,128)S(1)} %fusion.75, f32[128]{0:T(128)S(1)} %copy-done.16, bf16[3,3,128,128]{3,2,1,0:T(8,128)(2,1)S(1)} %copy-done.9, bf16[16,130,1,128]{3,0,2,1:T(8,128)(2,1)} %collective-permute-done.5, bf16[16,1,4,128]{3,0,2,1:T(8,128)(2,1)S(1)} %collective-permute-done.3, ...), kind=kOutput, calls=%fused_computation.6 | convolution fusion | flops 2426503168 | bytes 9781760 | tf_op jit(solution)/shard_map/conv_general_dilated | solution.py:34
  126.8 2.3 %collective-permute-start.6 = (bf16[16,1,4,128]{3,0,2,1:T(8,128)(2,1)S(1)}, bf16[16,1,4,128]{3,0,2,1:T(8,128)(2,1)S(1)}, u32[]{:S(2)}, u32[]{:S(2)}) collective-permute-start(bf16[16,1,4,128]{3,0,2,1:T(8,128)(2,1)S(1)} %slice.80), channel_id=1, source_target_pairs={{0,1},{1,2},{2,3},{4,5},{5,6},{6,7},{8,9},{9,10},{10,11},{12,13},{... | collective-permute-start | bytes 49160 | tf_op jit(solution)/shard_map/ppermute | solution.py:10
  129.2 0.9 collective-permute-done.6
  130.1 4.5 %collective-permute-start.7 = (bf16[16,129,1,128]{3,0,2,1:T(8,128)(2,1)S(1)}, bf16[16,129,1,128]{3,0,2,1:T(8,128)(2,1)S(1)}, u32[]{:S(2)}, u32[]{:S(2)}) collective-permute-start(bf16[16,129,1,128]{3,0,2,1:T(8,128)(2,1)S(1)} %pad_maximum_fusion.6), channel_id=1, source_target_pairs={{0,4},{4,8},{8,12},{1,5},{5,9},{9,13},{2,6},{6,10},{10,14},{3,7},{... | collective-permute-start | bytes 1585160 | tf_op jit(solution)/shard_map/ppermute | solution.py:10
  134.6 11.2 %collective-permute-done.7 = bf16[16,129,1,128]{3,0,2,1:T(8,128)(2,1)S(1)} collective-permute-done((bf16[16,129,1,128]{3,0,2,1:T(8,128)(2,1)S(1)}, bf16[16,129,1,128]{3,0,2,1:T(8,128)(2,1)S(1)}, u32[]{:S(2)}, u32[]{:S(2)}) %collective-permute-start.7) | collective-permute-done | bytes 528416 | tf_op jit(solution)/shard_map/ppermute | solution.py:10
  145.8 1.5 maximum_convert_fusion.3
  147.4 2.5 %collective-permute-start.8 = (bf16[16,1,2,256]{3,0,2,1:T(8,128)(2,1)S(1)}, bf16[16,1,2,256]{3,0,2,1:T(8,128)(2,1)S(1)}, u32[]{:S(2)}, u32[]{:S(2)}) collective-permute-start(bf16[16,1,2,256]{3,0,2,1:T(8,128)(2,1)S(1)} %get-tuple-element.11), channel_id=1, source_target_pairs={{0,1},{1,2},{2,3},{4,5},{5,6},{6,7},{8,9},{9,10},{10,11},{12,13},{... | collective-permute-start | bytes 49160 | tf_op jit(solution)/shard_map/ppermute | solution.py:10
  149.9 2.1 collective-permute-start.9
  152.0 3.1 %collective-permute-done.9 = bf16[16,1,2,256]{3,0,2,1:T(8,128)(2,1)S(1)} collective-permute-done((bf16[16,1,2,256]{3,0,2,1:T(8,128)(2,1)S(1)}, bf16[16,1,2,256]{3,0,2,1:T(8,128)(2,1)S(1)}, u32[]{:S(2)}, u32[]{:S(2)}) %collective-permute-start.9) | collective-permute-done | bytes 16416 | tf_op jit(solution)/shard_map/ppermute | solution.py:14
  155.3 4.3 %collective-permute-start.10 = (bf16[16,66,1,256]{3,0,2,1:T(8,128)(2,1)S(1)}, bf16[16,66,1,256]{3,0,2,1:T(8,128)(2,1)S(1)}, u32[]{:S(2)}, u32[]{:S(2)}) collective-permute-start(bf16[16,66,1,256]{3,0,2,1:T(8,128)(2,1)S(1)} %get-tuple-element.9), channel_id=1, source_target_pairs={{0,4},{4,8},{8,12},{1,5},{5,9},{9,13},{2,6},{6,10},{10,14},{3,7},{... | collective-permute-start | bytes 1622024 | tf_op jit(solution)/shard_map/ppermute | solution.py:10
  159.6 1.3 collective-permute-start.11
  160.9 0.4 fusion.69
  161.4 8.8 %collective-permute-done.10 = bf16[16,66,1,256]{3,0,2,1:T(8,128)(2,1)S(1)} collective-permute-done((bf16[16,66,1,256]{3,0,2,1:T(8,128)(2,1)S(1)}, bf16[16,66,1,256]{3,0,2,1:T(8,128)(2,1)S(1)}, u32[]{:S(2)}, u32[]{:S(2)}) %collective-permute-start.10) | collective-permute-done | bytes 540704 | tf_op jit(solution)/shard_map/ppermute | solution.py:10
  170.1 4.2 %collective-permute-done.11 = bf16[16,66,1,256]{3,0,2,1:T(8,128)(2,1)S(1)} collective-permute-done((bf16[16,66,1,256]{3,0,2,1:T(8,128)(2,1)S(1)}, bf16[16,66,1,256]{3,0,2,1:T(8,128)(2,1)S(1)}, u32[]{:S(2)}, u32[]{:S(2)}) %collective-permute-start.11) | collective-permute-done | bytes 540704 | tf_op jit(solution)/shard_map/ppermute | solution.py:14
  174.3 2.7 %maximum_convert_fusion.2 = bf16[16,64,2,256]{3,0,2,1:T(8,128)(2,1)S(1)} fusion(f32[16,64,2,256]{3,0,2,1:T(8,128)S(1)} %fusion.69, bf16[3,3,256,256]{3,2,1,0:T(8,128)(2,1)S(1)} %copy-done.7, bf16[16,66,1,256]{3,0,2,1:T(8,128)(2,1)S(1)} %collective-permute-done.11, bf16[16,1,2,256]{3,0,2,1:T(8,128)(2,1)S(1)} %collective-permute-done.9, ...), kind=kOutput, calls=%fused_computation.34 | convolution fusion | flops 2422341632 | bytes 6489088 | tf_op jit(solution)/shard_map/conv_general_dilated | solution.py:34
  177.0 1.9 collective-permute-start.12
  179.0 1.1 collective-permute-done.12
  180.2 2.9 %collective-permute-start.13 = (bf16[16,65,1,256]{3,0,2,1:T(8,128)(2,1)S(1)}, bf16[16,65,1,256]{3,0,2,1:T(8,128)(2,1)S(1)}, u32[]{:S(2)}, u32[]{:S(2)}) collective-permute-start(bf16[16,65,1,256]{3,0,2,1:T(8,128)(2,1)S(1)} %pad_maximum_fusion.2), channel_id=1, source_target_pairs={{0,4},{4,8},{8,12},{1,5},{5,9},{9,13},{2,6},{6,10},{10,14},{3,7},{... | collective-permute-start | bytes 1597448 | tf_op jit(solution)/shard_map/ppermute | solution.py:10
  183.1 11.2 %collective-permute-done.13 = bf16[16,65,1,256]{3,0,2,1:T(8,128)(2,1)S(1)} collective-permute-done((bf16[16,65,1,256]{3,0,2,1:T(8,128)(2,1)S(1)}, bf16[16,65,1,256]{3,0,2,1:T(8,128)(2,1)S(1)}, u32[]{:S(2)}, u32[]{:S(2)}) %collective-permute-start.13) | collective-permute-done | bytes 532512 | tf_op jit(solution)/shard_map/ppermute | solution.py:10
  194.3 1.4 fusion.66
  195.7 2.3 %collective-permute-start.14 = (bf16[16,1,1,320]{3,0,2,1:T(8,128)(2,1)S(1)}, bf16[16,1,1,320]{3,0,2,1:T(8,128)(2,1)S(1)}, u32[]{:S(2)}, u32[]{:S(2)}) collective-permute-start(bf16[16,1,1,320]{3,0,2,1:T(8,128)(2,1)S(1)} %get-tuple-element.13), channel_id=1, source_target_pairs={{0,1},{1,2},{2,3},{4,5},{5,6},{6,7},{8,9},{9,10},{10,11},{12,13},{... | collective-permute-start | bytes 30728 | tf_op jit(solution)/shard_map/ppermute | solution.py:10
  198.1 2.0 collective-permute-start.15
  200.1 3.0 %collective-permute-done.15 = bf16[16,1,1,320]{3,0,2,1:T(8,128)(2,1)S(1)} collective-permute-done((bf16[16,1,1,320]{3,0,2,1:T(8,128)(2,1)S(1)}, bf16[16,1,1,320]{3,0,2,1:T(8,128)(2,1)S(1)}, u32[]{:S(2)}, u32[]{:S(2)}) %collective-permute-start.15) | collective-permute-done | bytes 10272 | tf_op jit(solution)/shard_map/ppermute | solution.py:14
  203.2 4.2 %collective-permute-start.16 = (bf16[16,34,1,320]{3,0,2,1:T(8,128)(2,1)S(1)}, bf16[16,34,1,320]{3,0,2,1:T(8,128)(2,1)S(1)}, u32[]{:S(2)}, u32[]{:S(2)}) collective-permute-start(bf16[16,34,1,320]{3,0,2,1:T(8,128)(2,1)S(1)} %pad_maximum_fusion.7), channel_id=1, source_target_pairs={{0,4},{4,8},{8,12},{1,5},{5,9},{9,13},{2,6},{6,10},{10,14},{3,7},{... | collective-permute-start | bytes 1044488 | tf_op jit(solution)/shard_map/ppermute | solution.py:10
  207.3 1.3 collective-permute-start.17
  209.0 6.4 %collective-permute-done.16 = bf16[16,34,1,320]{3,0,2,1:T(8,128)(2,1)S(1)} collective-permute-done((bf16[16,34,1,320]{3,0,2,1:T(8,128)(2,1)S(1)}, bf16[16,34,1,320]{3,0,2,1:T(8,128)(2,1)S(1)}, u32[]{:S(2)}, u32[]{:S(2)}) %collective-permute-start.16) | collective-permute-done | bytes 348192 | tf_op jit(solution)/shard_map/ppermute | solution.py:10
  215.4 4.1 %collective-permute-done.17 = bf16[16,34,1,320]{3,0,2,1:T(8,128)(2,1)S(1)} collective-permute-done((bf16[16,34,1,320]{3,0,2,1:T(8,128)(2,1)S(1)}, bf16[16,34,1,320]{3,0,2,1:T(8,128)(2,1)S(1)}, u32[]{:S(2)}, u32[]{:S(2)}) %collective-permute-start.17) | collective-permute-done | bytes 348192 | tf_op jit(solution)/shard_map/ppermute | solution.py:14
  219.5 1.8 fusion.63
  221.4 0.8 copy.34
  (50 shorter events, 0.9 us)
Async XLA Ops:
  0.0 219.5 %copy-start = (bf16[3,3,320,320]{3,2,1,0:T(8,128)(2,1)S(1)}, bf16[3,3,320,320]{3,2,1,0:T(8,128)(2,1)}, u32[]{:S(2)}) copy-start(bf16[3,3,320,320]{3,2,1,0:T(8,128)(2,1)} %param.29) | copy-start | bytes 5529604
  13.9 5.5 %collective-permute-start = (bf16[16,1,8,64]{3,0,2,1:T(8,128)(2,1)S(1)}, bf16[16,1,8,64]{3,0,2,1:T(8,128)(2,1)S(1)}, u32[]{:S(2)}, u32[]{:S(2)}) collective-permute-start(bf16[16,1,8,64]{3,0,2,1:T(8,128)(2,1)S(1)} %slice.77), channel_id=1, source_target_pairs={{0,1},{1,2},{2,3},{4,5},{5,6},{6,7},{8,9},{9,10},{10,11},{12,13},{... | collective-permute-start | bytes 49160 | tf_op jit(solution)/shard_map/ppermute | solution.py:10
  20.9 23.1 %copy-start.10 = (bf16[3,3,64,128]{3,2,1,0:T(8,128)(2,1)S(1)}, bf16[3,3,64,128]{3,2,1,0:T(8,128)(2,1)}, u32[]{:S(2)}) copy-start(bf16[3,3,64,128]{3,2,1,0:T(8,128)(2,1)} %param.17) | copy-start | bytes 442372
  20.9 23.1 %copy-start.15 = (f32[128]{0:T(128)S(1)}, f32[128]{0:T(128)}, u32[]{:S(2)}) copy-start(f32[128]{0:T(128)} %param.18) | copy-start | bytes 1540
  22.6 19.5 %collective-permute-start.1 = (bf16[16,257,1,64]{1,3,2,0:T(8,128)(2,1)}, bf16[16,257,1,64]{1,3,2,0:T(8,128)(2,1)}, u32[]{:S(2)}, u32[]{:S(2)}) collective-permute-start(bf16[16,257,1,64]{1,3,2,0:T(8,128)(2,1)} %copy.27), channel_id=1, source_target_pairs={{0,4},{4,8},{8,12},{1,5},{5,9},{9,13},{2,6},{6,10},{10,14},{3,7},{... | collective-permute-start | bytes 1579016 | tf_op jit(solution)/shard_map/ppermute | solution.py:10
  51.0 14.2 %copy-start.1 = (bf16[16,128,4,128]{3,0,2,1:T(8,128)(2,1)}, bf16[16,128,4,128]{3,0,2,1:T(8,128)(2,1)S(1)}, u32[]{:S(2)}) copy-start(bf16[16,128,4,128]{3,0,2,1:T(8,128)(2,1)S(1)} %maximum_convert_fusion.1) | copy-start | bytes 6291460
  51.1 4.9 %collective-permute-start.2 = (bf16[16,1,4,128]{3,0,2,1:T(8,128)(2,1)S(1)}, bf16[16,1,4,128]{3,0,2,1:T(8,128)(2,1)S(1)}, u32[]{:S(2)}, u32[]{:S(2)}) collective-permute-start(bf16[16,1,4,128]{3,0,2,1:T(8,128)(2,1)S(1)} %get-tuple-element.7), channel_id=1, source_target_pairs={{0,1},{1,2},{2,3},{4,5},{5,6},{6,7},{8,9},{9,10},{10,11},{12,13},{... | collective-permute-start | bytes 49160 | tf_op jit(solution)/shard_map/ppermute | solution.py:10
  54.1 5.1 %collective-permute-start.3 = (bf16[16,1,4,128]{3,0,2,1:T(8,128)(2,1)S(1)}, bf16[16,1,4,128]{3,0,2,1:T(8,128)(2,1)S(1)}, u32[]{:S(2)}, u32[]{:S(2)}) collective-permute-start(bf16[16,1,4,128]{3,0,2,1:T(8,128)(2,1)S(1)} %get-tuple-element.8), channel_id=1, source_target_pairs={{1,0},{2,1},{3,2},{5,4},{6,5},{7,6},{9,8},{10,9},{11,10},{13,12},{... | collective-permute-start | bytes 49160 | tf_op jit(solution)/shard_map/ppermute | solution.py:14
  60.3 60.0 %collective-permute-start.4 = (bf16[16,130,1,128]{3,0,2,1:T(8,128)(2,1)}, bf16[16,130,1,128]{3,0,2,1:T(8,128)(2,1)}, u32[]{:S(2)}, u32[]{:S(2)}) collective-permute-start(bf16[16,130,1,128]{3,0,2,1:T(8,128)(2,1)} %get-tuple-element.5), channel_id=1, source_target_pairs={{0,4},{4,8},{8,12},{1,5},{5,9},{9,13},{2,6},{6,10},{10,14},{3,7},{... | collective-permute-start | bytes 1597448 | tf_op jit(solution)/shard_map/ppermute | solution.py:10
  65.2 55.1 %collective-permute-start.5 = (bf16[16,130,1,128]{3,0,2,1:T(8,128)(2,1)}, bf16[16,130,1,128]{3,0,2,1:T(8,128)(2,1)}, u32[]{:S(2)}, u32[]{:S(2)}) collective-permute-start(bf16[16,130,1,128]{3,0,2,1:T(8,128)(2,1)} %get-tuple-element.6), channel_id=1, source_target_pairs={{4,0},{8,4},{12,8},{5,1},{9,5},{13,9},{6,2},{10,6},{14,10},{7,3},{... | collective-permute-start | bytes 1597448 | tf_op jit(solution)/shard_map/ppermute | solution.py:14
  114.1 3.7 %copy-start.5 = (bf16[64,128]{1,0:T(8,128)(2,1)S(1)}, bf16[64,128]{1,0:T(8,128)(2,1)}, u32[]{:S(2)}) copy-start(bf16[64,128]{1,0:T(8,128)(2,1)} %param.21) | copy-start | bytes 49156
  117.8 2.5 %copy-start.2 = (bf16[16,128,4,128]{3,0,2,1:T(8,128)(2,1)S(1)}, bf16[16,128,4,128]{3,0,2,1:T(8,128)(2,1)}, u32[]{:S(2)}) copy-start(bf16[16,128,4,128]{3,0,2,1:T(8,128)(2,1)} %copy-done.1) | copy-start | bytes 6291460
  117.8 2.5 %copy-start.9 = (bf16[3,3,128,128]{3,2,1,0:T(8,128)(2,1)S(1)}, bf16[3,3,128,128]{3,2,1,0:T(8,128)(2,1)}, u32[]{:S(2)}) copy-start(bf16[3,3,128,128]{3,2,1,0:T(8,128)(2,1)} %param.19) | copy-start | bytes 884740
  117.8 2.5 %copy-start.16 = (f32[128]{0:T(128)S(1)}, f32[128]{0:T(128)}, u32[]{:S(2)}) copy-start(f32[128]{0:T(128)} %param.20) | copy-start | bytes 1540
  126.8 19.0 %copy-start.8 = (bf16[3,3,128,256]{3,2,1,0:T(8,128)(2,1)S(1)}, bf16[3,3,128,256]{3,2,1,0:T(8,128)(2,1)}, u32[]{:S(2)}) copy-start(bf16[3,3,128,256]{3,2,1,0:T(8,128)(2,1)} %param.22) | copy-start | bytes 1769476
  126.8 19.0 %copy-start.13 = (f32[256]{0:T(256)S(1)}, f32[256]{0:T(256)}, u32[]{:S(2)}) copy-start(f32[256]{0:T(256)} %param.23) | copy-start | bytes 3076
  126.8 3.2 %collective-permute-start.6 = (bf16[16,1,4,128]{3,0,2,1:T(8,128)(2,1)S(1)}, bf16[16,1,4,128]{3,0,2,1:T(8,128)(2,1)S(1)}, u32[]{:S(2)}, u32[]{:S(2)}) collective-permute-start(bf16[16,1,4,128]{3,0,2,1:T(8,128)(2,1)S(1)} %slice.80), channel_id=1, source_target_pairs={{0,1},{1,2},{2,3},{4,5},{5,6},{6,7},{8,9},{9,10},{10,11},{12,13},{... | collective-permute-start | bytes 49160 | tf_op jit(solution)/shard_map/ppermute | solution.py:10
  130.1 15.7 %collective-permute-start.7 = (bf16[16,129,1,128]{3,0,2,1:T(8,128)(2,1)S(1)}, bf16[16,129,1,128]{3,0,2,1:T(8,128)(2,1)S(1)}, u32[]{:S(2)}, u32[]{:S(2)}) collective-permute-start(bf16[16,129,1,128]{3,0,2,1:T(8,128)(2,1)S(1)} %pad_maximum_fusion.6), channel_id=1, source_target_pairs={{0,4},{4,8},{8,12},{1,5},{5,9},{9,13},{2,6},{6,10},{10,14},{3,7},{... | collective-permute-start | bytes 1585160 | tf_op jit(solution)/shard_map/ppermute | solution.py:10
  147.4 4.6 %collective-permute-start.8 = (bf16[16,1,2,256]{3,0,2,1:T(8,128)(2,1)S(1)}, bf16[16,1,2,256]{3,0,2,1:T(8,128)(2,1)S(1)}, u32[]{:S(2)}, u32[]{:S(2)}) collective-permute-start(bf16[16,1,2,256]{3,0,2,1:T(8,128)(2,1)S(1)} %get-tuple-element.11), channel_id=1, source_target_pairs={{0,1},{1,2},{2,3},{4,5},{5,6},{6,7},{8,9},{9,10},{10,11},{12,13},{... | collective-permute-start | bytes 49160 | tf_op jit(solution)/shard_map/ppermute | solution.py:10
  149.9 11.1 %copy-start.4 = (bf16[128,256]{1,0:T(8,128)(2,1)S(1)}, bf16[128,256]{1,0:T(8,128)(2,1)}, u32[]{:S(2)}) copy-start(bf16[128,256]{1,0:T(8,128)(2,1)} %param.26) | copy-start | bytes 196612
  149.9 5.2 %collective-permute-start.9 = (bf16[16,1,2,256]{3,0,2,1:T(8,128)(2,1)S(1)}, bf16[16,1,2,256]{3,0,2,1:T(8,128)(2,1)S(1)}, u32[]{:S(2)}, u32[]{:S(2)}) collective-permute-start(bf16[16,1,2,256]{3,0,2,1:T(8,128)(2,1)S(1)} %get-tuple-element.12), channel_id=1, source_target_pairs={{1,0},{2,1},{3,2},{5,4},{6,5},{7,6},{9,8},{10,9},{11,10},{13,12},{... | collective-permute-start | bytes 49160 | tf_op jit(solution)/shard_map/ppermute | solution.py:14
  155.2 19.1 %copy-start.7 = (bf16[3,3,256,256]{3,2,1,0:T(8,128)(2,1)S(1)}, bf16[3,3,256,256]{3,2,1,0:T(8,128)(2,1)}, u32[]{:S(2)}) copy-start(bf16[3,3,256,256]{3,2,1,0:T(8,128)(2,1)} %param.24) | copy-start | bytes 3538948
  155.2 19.1 %copy-start.14 = (f32[256]{0:T(256)S(1)}, f32[256]{0:T(256)}, u32[]{:S(2)}) copy-start(f32[256]{0:T(256)} %param.25) | copy-start | bytes 3076
  155.3 14.8 %collective-permute-start.10 = (bf16[16,66,1,256]{3,0,2,1:T(8,128)(2,1)S(1)}, bf16[16,66,1,256]{3,0,2,1:T(8,128)(2,1)S(1)}, u32[]{:S(2)}, u32[]{:S(2)}) collective-permute-start(bf16[16,66,1,256]{3,0,2,1:T(8,128)(2,1)S(1)} %get-tuple-element.9), channel_id=1, source_target_pairs={{0,4},{4,8},{8,12},{1,5},{5,9},{9,13},{2,6},{6,10},{10,14},{3,7},{... | collective-permute-start | bytes 1622024 | tf_op jit(solution)/shard_map/ppermute | solution.py:10
  159.6 14.7 %collective-permute-start.11 = (bf16[16,66,1,256]{3,0,2,1:T(8,128)(2,1)S(1)}, bf16[16,66,1,256]{3,0,2,1:T(8,128)(2,1)S(1)}, u32[]{:S(2)}, u32[]{:S(2)}) collective-permute-start(bf16[16,66,1,256]{3,0,2,1:T(8,128)(2,1)S(1)} %get-tuple-element.10), channel_id=1, source_target_pairs={{4,0},{8,4},{12,8},{5,1},{9,5},{13,9},{6,2},{10,6},{14,10},{7,3},{... | collective-permute-start | bytes 1622024 | tf_op jit(solution)/shard_map/ppermute | solution.py:14
  161.3 32.9 %copy-start.6 = (bf16[3,3,256,320]{2,3,1,0:T(8,128)(2,1)S(1)}, bf16[3,3,256,320]{2,3,1,0:T(8,128)(2,1)}, u32[]{:S(2)}) copy-start(bf16[3,3,256,320]{2,3,1,0:T(8,128)(2,1)} %param.27) | copy-start | bytes 4423684
  161.4 32.9 %copy-start.11 = (f32[320]{0:T(512)S(1)}, f32[320]{0:T(512)}, u32[]{:S(2)}) copy-start(f32[320]{0:T(512)} %param.28) | copy-start | bytes 3844
  177.0 3.1 %collective-permute-start.12 = (bf16[16,1,2,256]{3,0,2,1:T(8,128)(2,1)S(1)}, bf16[16,1,2,256]{3,0,2,1:T(8,128)(2,1)S(1)}, u32[]{:S(2)}, u32[]{:S(2)}) collective-permute-start(bf16[16,1,2,256]{3,0,2,1:T(8,128)(2,1)S(1)} %slice.85), channel_id=1, source_target_pairs={{0,1},{1,2},{2,3},{4,5},{5,6},{6,7},{8,9},{9,10},{10,11},{12,13},{... | collective-permute-start | bytes 49160 | tf_op jit(solution)/shard_map/ppermute | solution.py:10
  180.2 28.5 %copy-start.3 = (bf16[256,320]{0,1:T(8,128)(2,1)S(1)}, bf16[256,320]{0,1:T(8,128)(2,1)}, u32[]{:S(2)}) copy-start(bf16[256,320]{0,1:T(8,128)(2,1)} %param.31) | copy-start | bytes 491524
  180.2 14.1 %collective-permute-start.13 = (bf16[16,65,1,256]{3,0,2,1:T(8,128)(2,1)S(1)}, bf16[16,65,1,256]{3,0,2,1:T(8,128)(2,1)S(1)}, u32[]{:S(2)}, u32[]{:S(2)}) collective-permute-start(bf16[16,65,1,256]{3,0,2,1:T(8,128)(2,1)S(1)} %pad_maximum_fusion.2), channel_id=1, source_target_pairs={{0,4},{4,8},{8,12},{1,5},{5,9},{9,13},{2,6},{6,10},{10,14},{3,7},{... | collective-permute-start | bytes 1597448 | tf_op jit(solution)/shard_map/ppermute | solution.py:10
  195.7 23.8 %copy-start.12 = (f32[320]{0:T(512)S(1)}, f32[320]{0:T(512)}, u32[]{:S(2)}) copy-start(f32[320]{0:T(512)} %param.30) | copy-start | bytes 3844
  195.7 4.3 %collective-permute-start.14 = (bf16[16,1,1,320]{3,0,2,1:T(8,128)(2,1)S(1)}, bf16[16,1,1,320]{3,0,2,1:T(8,128)(2,1)S(1)}, u32[]{:S(2)}, u32[]{:S(2)}) collective-permute-start(bf16[16,1,1,320]{3,0,2,1:T(8,128)(2,1)S(1)} %get-tuple-element.13), channel_id=1, source_target_pairs={{0,1},{1,2},{2,3},{4,5},{5,6},{6,7},{8,9},{9,10},{10,11},{12,13},{... | collective-permute-start | bytes 30728 | tf_op jit(solution)/shard_map/ppermute | solution.py:10
  198.1 5.0 %collective-permute-start.15 = (bf16[16,1,1,320]{3,0,2,1:T(8,128)(2,1)S(1)}, bf16[16,1,1,320]{3,0,2,1:T(8,128)(2,1)S(1)}, u32[]{:S(2)}, u32[]{:S(2)}) collective-permute-start(bf16[16,1,1,320]{3,0,2,1:T(8,128)(2,1)S(1)} %get-tuple-element.14), channel_id=1, source_target_pairs={{1,0},{2,1},{3,2},{5,4},{6,5},{7,6},{9,8},{10,9},{11,10},{13,12},{... | collective-permute-start | bytes 30728 | tf_op jit(solution)/shard_map/ppermute | solution.py:14
  203.2 12.2 %collective-permute-start.16 = (bf16[16,34,1,320]{3,0,2,1:T(8,128)(2,1)S(1)}, bf16[16,34,1,320]{3,0,2,1:T(8,128)(2,1)S(1)}, u32[]{:S(2)}, u32[]{:S(2)}) collective-permute-start(bf16[16,34,1,320]{3,0,2,1:T(8,128)(2,1)S(1)} %pad_maximum_fusion.7), channel_id=1, source_target_pairs={{0,4},{4,8},{8,12},{1,5},{5,9},{9,13},{2,6},{6,10},{10,14},{3,7},{... | collective-permute-start | bytes 1044488 | tf_op jit(solution)/shard_map/ppermute | solution.py:10
  207.3 12.2 %collective-permute-start.17 = (bf16[16,34,1,320]{3,0,2,1:T(8,128)(2,1)S(1)}, bf16[16,34,1,320]{3,0,2,1:T(8,128)(2,1)S(1)}, u32[]{:S(2)}, u32[]{:S(2)}) collective-permute-start(bf16[16,34,1,320]{3,0,2,1:T(8,128)(2,1)S(1)} %pad_maximum_fusion.7), channel_id=1, source_target_pairs={{4,0},{8,4},{12,8},{5,1},{9,5},{13,9},{6,2},{10,6},{14,10},{7,3},{... | collective-permute-start | bytes 1044488 | tf_op jit(solution)/shard_map/ppermute | solution.py:14
where the time goes:
time: 226 us; the launch traced here: 222 us
  waiting for transfers between devices  73.6 us (33%)
  local copies, waits for them, and re-layouts  69.8 us (31%)
  starting transfers between devices  51.2 us (23%)
  matrix products  24.1 us (11%)
  other arithmetic  2.97 us (1%)
    ppermute x12, waiting for transfers between devices, from_lower(): lax.ppermute(edge_part, axis_name, [(dev_index, dev_index + 1) for dev_in...  56.1 us
    slice x2, local copies, waits for them, and re-layouts, basic_block(): z_prev[:, ::2, ::2]  51.3 us
    ppermute x12, starting transfers between devices, from_lower(): lax.ppermute(edge_part, axis_name, [(dev_index, dev_index + 1) for dev_in...  41.4 us
    conv_general_dilated x6, matrix products, conv_valid(): lax.conv_general_dilated(act_in, weight, (stride, stride), 'VALID', dimen...  21 us
    ppermute x6, waiting for transfers between devices, from_upper(): lax.ppermute(edge_part, axis_name, [(dev_index + 1, dev_index) for dev_in...  17.5 us
    unnamed x35, local copies, waits for them, and re-layouts  13.3 us
    ppermute x6, starting transfers between devices, from_upper(): lax.ppermute(edge_part, axis_name, [(dev_index + 1, dev_index) for dev_in...  9.85 us
  transfers between devices with their start and end apart: 18, of which 13 were waited for; matrix products, arithmetic and copies ran while one was open for 25% of the time, Pallas kernels for 0%

commit v1 on v0

v1 whole, which is shorter than its diff:
```python
import functools

import jax
import jax.numpy as jnp
from jax import lax
from jax.experimental import pallas as pl
from jax.experimental.pallas import tpu as pltpu
from jax.sharding import PartitionSpec as P

BF16 = jnp.bfloat16
F32 = jnp.float32
SHIFTS = (0, 1)
NCH = 4
NCH3 = 2
PAIRS = 4
MAX_PLAN = 5
OWN, HALO = range(2)
NT = (((1,), (1,)), ((), ()))


def loop(count, body):
    lax.fori_loop(0, count, body, 0)


def row_plan(kind, width, s_send, s_recv):
    if kind == "x":
        own = (0, width - 1)
        need = (-1, width - 1) if s_recv == 0 else (0, width)
        src_at, dst_at = 2 - s_send, 2 - s_recv
    elif kind == "y":
        own = (s_send, width - 1 + s_send)
        need = (s_recv - 1, s_recv + width)
        src_at, dst_at = 2 - s_send, 2 - s_recv
    else:
        own = (s_send, width - 1 + s_send)
        need = (-1, width - 1) if s_recv == 0 else (0, width + 1)
        src_at, dst_at = 3 - 2 * s_send, 3 - 2 * s_recv
    plan = []
    for dist in range(-2, 3):
        lo = max(own[0], width * dist + need[0])
        hi = min(own[1], width * dist + need[1])
        if lo <= hi:
            plan.append((dist, lo + src_at, lo - width * dist + dst_at, hi - lo + 1, False))
        if kind != "x" and s_send == 1 and s_recv == 0 and dist >= 0 and need[0] + width * dist <= 0 <= need[1] + width * dist:
            plan.append((dist, src_at, dst_at - width * dist, 1, True))
    return plan


def kernel(dims, x_hbm, w1d_h, w1c_h, wp1_h, w2d_h, w2c_h, wp2_h, w3d_h, w3c_h, wp3_h, b1d_h, b1c_h, b2d_h, b2c_h, b3d_h, b3c_h, out_hbm,
           raw, xh, stage_f, eye, xs, y1, z1, y2, z2, y3, zo, w1d, w1c, w2d, w2c, w3r, w3d, w3c, wp3r, wp3,
           b1d, b1c, b2d, b2c, b3d, b3c, load_sem, x_sem, col_send, col_recv, row_send, row_recv, out_sem):
    n, h, c0, c1, c2, c3, rows, cols = dims
    h4, h8 = h // 4, h // 8
    ch, ch3 = h4 // NCH, h8 // NCH3
    hh = h // 2
    row = lax.axis_index("row")
    col = lax.axis_index("col")
    s = lax.rem(row, 2)
    is0 = s == 0
    first_extra = (s == 1) & (col == 0)
    last_void = (s == 1) & (col == cols - 1)
    t_first = jnp.where(first_extra, -1, 0)
    fwd_col = jnp.where(is0, col + 1, col - 1)
    bwd_col = jnp.where(is0, col - 1, col + 1)
    has_fwd = (fwd_col >= 0) & (fwd_col < cols)
    has_bwd = (bwd_col >= 0) & (bwd_col < cols)

    load_count = []

    def load(src, dst):
        load_count.append(dst)
        return pltpu.make_async_copy(src, dst, load_sem.at[len(load_count) - 1])

    k1, k2 = 9 * c1, 9 * c2
    pair = 2 * c0
    x_loads = [load(x_hbm.at[:, q], raw.at[q]) for q in range(PAIRS)]
    w1d_loads = [load(b1d_h, b1d), load(b1c_h, b1c)]
    w1c_loads = []
    for p in range(2):
        lanes = pl.ds(p * c1, c1)
        for kh in range(3):
            w1d_loads.append(load(w1d_h.at[kh], w1d.at[pl.ds((kh + 2 * p) * 2 * pair + c0, 3 * c0), lanes]))
        w1c_loads.append(load(w1c_h, w1c.at[pl.ds(p * 3 * c1, k1), lanes]))
        w1c_loads.append(load(wp1_h, w1c.at[pl.ds(12 * c1 + p * pair, c0), lanes]))
    w2d_loads = [load(w2d_h, w2d), load(b2d_h, b2d)]
    w2c_loads = [load(w2c_h, w2c.at[pl.ds(0, k2)]), load(wp2_h, w2c.at[pl.ds(k2, c1)]), load(b2c_h, b2c)]
    w3d_loads = [load(w3d_h, w3r), load(b3d_h, b3d), load(wp3_h, wp3r)]
    w3c_loads = [load(w3c_h, w3c), load(b3c_h, b3c)]
    for copy in x_loads + w1d_loads + w1c_loads + w2d_loads + w2c_loads + w3d_loads + w3c_loads:
        copy.start()

    def row_refs(name, slots, down, side):
        ref = refs[name]
        last = ref.shape[1] - (2 if ROW_SEM[name][0] == "y" else 1)
        own_at, halo_at = (last, 0) if down else (1, last + 1)
        at = own_at if side == OWN else halo_at
        subs = 1 if len(ref.shape) == 4 else ref.shape[2]
        if subs == 1:
            return ref.at[slots, at]
        return ref.at[slots, at, subs - 1 if down else 0]

    refs = dict(x=xs, y1=y1, z1=z1, y2=y2, z2=z2, y3=y3)
    ROW_SEM = {}
    for name, kind, width in (("x", "x", PAIRS), ("y1", "y", PAIRS), ("z1", "z", PAIRS), ("y2", "y", 2), ("z2", "z", 2), ("y3", "y", 1)):
        ROW_SEM[name] = (kind, width, 2 * MAX_PLAN * len(ROW_SEM))

    def directions(name):
        return (True, False) if ROW_SEM[name][0] == "y" else (True,)

    def zero_slot(ref, idx):
        def body(i, carry):
            ref[idx, i] = jnp.zeros(ref.shape[2:], ref.dtype)
            return carry
        loop(ref.shape[1], body)

    for name in ROW_SEM:
        for down in directions(name):
            edge = row_refs(name, slice(None), down, HALO)
            edge[...] = jnp.zeros(edge.shape, BF16)

    @pl.when(col == 0)
    def _():
        for slots, group in enumerate(((xs, y1, z1, y2, z2, y3), (y1, z1, y2, z2, y3), (z1, z2))):
            for ref in group:
                zero_slot(ref, slots)

    @pl.when(col == cols - 1)
    def _():
        for ref in (y1, z1, y2, z2, y3):
            zero_slot(ref, ref.shape[0] - 1)

    @pl.when(is0 | jnp.logical_not(has_bwd))
    def _():
        def body(i, carry):
            xh[0, i] = jnp.zeros((2 * c0, hh), BF16)
            xh[1, i] = jnp.zeros((2 * c0, hh), BF16)
            return carry
        loop(n, body)

    barrier = pltpu.get_barrier_semaphore()
    for rr in range(rows):
        for cc in range(cols):
            pl.semaphore_signal(barrier, inc=1, device_id={"row": jnp.int32(rr), "col": jnp.int32(cc)}, device_id_type=pl.DeviceIdType.MESH)
    pl.semaphore_wait(barrier, rows * cols)

    def remote(src, dst, send_sem, recv_sem, to_row, to_col):
        return pltpu.make_async_remote_copy(src_ref=src, dst_ref=dst, send_sem=send_sem, recv_sem=recv_sem,
                                            device_id={"row": to_row, "col": to_col}, device_id_type=pl.DeviceIdType.MESH)

    def x_copy(shift, half):
        lanes = pl.ds(half * hh, hh)
        if shift == 0:
            src, dst = x_hbm.at[:, 3, pl.ds(c0, c0), lanes], xh.at[half, :, pl.ds(c0, c0)]
        else:
            src, dst = x_hbm.at[:, 0, :, lanes], xh.at[half]
        return remote(src, dst, x_sem.at[half], x_sem.at[2 + half], row, fwd_col)

    for shift in SHIFTS:
        @pl.when(has_fwd & (s == shift))
        def _():
            for half in range(2):
                x_copy(shift, half).start()

    def y_copy(ref, width, rows_per, sem0, forward, chunk, nch):
        to_right = is0 if forward else jnp.logical_not(is0)
        src_slot = jnp.where(to_right, width + 1, 2)
        dst_slot = jnp.where(to_right, 1, width + 2)
        part = pl.ds(1 + chunk * rows_per, rows_per)
        sem = sem0 + (0 if forward else nch) + chunk
        return remote(ref.at[src_slot, part], ref.at[dst_slot, part], col_send.at[sem], col_recv.at[sem], row, fwd_col if forward else bwd_col)

    def y_recv(ref, width, rows_per, sem0, forward, chunk, nch):
        to_right = is0 if forward else jnp.logical_not(is0)
        dst_slot = jnp.where(to_right, 1, width + 2)
        part = pl.ds(1 + chunk * rows_per, rows_per)
        sem = sem0 + (0 if forward else nch) + chunk
        return remote(ref.at[dst_slot, part], ref.at[dst_slot, part], col_send.at[sem], col_recv.at[sem], row, bwd_col if forward else fwd_col)

    def z_copy(ref, width, rows_per, sem0, chunk):
        src_slot = jnp.where(is0, width + 2, 2)
        dst_slot = jnp.where(is0, 2, width + 2)
        part = pl.ds(1 + chunk * rows_per, rows_per)
        sem = sem0 + chunk
        return remote(ref.at[src_slot, part], ref.at[dst_slot, part], col_send.at[sem], col_recv.at[sem], row, fwd_col)

    def z_recv(ref, width, rows_per, sem0, chunk):
        dst_slot = jnp.where(is0, 2, width + 2)
        part = pl.ds(1 + chunk * rows_per, rows_per)
        sem = sem0 + chunk
        return remote(ref.at[dst_slot, part], ref.at[dst_slot, part], col_send.at[sem], col_recv.at[sem], row, bwd_col)

    SEM_Y1, SEM_Z1, SEM_Y2, SEM_Z2, SEM_Y3 = (i * 2 * NCH for i in range(5))

    def row_messages(name, act):
        kind, width, sem0 = ROW_SEM[name]
        for down in directions(name):
            for s_send, s_recv in zip(SHIFTS, reversed(SHIFTS)):
                step = 1 if down else -1
                for i, (dist, src, dst, count, extra) in enumerate(row_plan(kind, width, s_send, s_recv)):
                    sem = sem0 + i + (0 if down else MAX_PLAN)
                    if act == "recv":
                        from_row, from_col = row - step, col - dist
                        ok = (s == s_recv) & (from_row >= 0) & (from_row < rows) & (from_col >= 0) & (from_col < cols)
                        if extra:
                            ok = ok & (from_col == 0)

                        @pl.when(ok)
                        def _():
                            ref = row_refs(name, pl.ds(dst, count), down, HALO)
                            remote(ref, ref, row_send.at[sem], row_recv.at[sem], from_row, from_col).wait_recv()
                    else:
                        to_row, to_col = row + step, col + dist
                        ok = (s == s_send) & (to_row >= 0) & (to_row < rows) & (to_col >= 0) & (to_col < cols)
                        if extra:
                            ok = ok & (col == 0)

                        @pl.when(ok)
                        def _():
                            copy = remote(row_refs(name, pl.ds(src, count), down, OWN), row_refs(name, pl.ds(dst, count), down, HALO),
                                          row_send.at[sem], row_recv.at[sem], to_row, to_col)
                            if act == "send":
                                copy.start()
                            else:
                                copy.wait_send()

    eye[...] = (lax.broadcasted_iota(jnp.int32, (h, h), 0) == lax.broadcasted_iota(jnp.int32, (h, h), 1)).astype(F32).astype(BF16)

    def transpose_pair(read, size, slot, h4_first):
        unit = eye[0:size, 0:size]

        def turn(i, carry):
            block = read(2 * i).reshape(2 * pair, size)
            turned = lax.dot_general(unit, block, NT, preferred_element_type=F32)
            for j in range(2):
                stage_f[pl.ds(2 * i + j, size, stride=n), :] = turned[:, j * pair:(j + 1) * pair]
            return carry
        loop(n // 2, turn)
        step = 4

        def pack(i, carry):
            part = stage_f[pl.ds(i * (step * 4 * n), step * 4 * n), :]
            xs[slot, pl.ds(h4_first + i * step, step)] = part.reshape(step, 4, n, 2 * c0).astype(BF16)
            return carry
        loop(size // 4 // step, pack)

    def zero_part(ref, first, size, p):
        ref[pl.ds(first, size), pl.ds(p * c1, c1)] = jnp.zeros((size, c1), BF16)

    def zero_weights():
        for p in range(2):
            for kh in range(5):
                tap_at = kh * 2 * pair
                used = 2 * p <= kh < 2 * p + 3
                zero_part(w1d, tap_at, c0 if used else 2 * pair, p)
            zero_part(w1c, (1 - p) * k1, 3 * c1, p)
            proj_at = 12 * c1
            zero_part(w1c, proj_at + (1 - p) * pair, pair, p)
            zero_part(w1c, proj_at + p * pair + c0, c0, p)

    zero_weights()
    for q in range(4):
        x_loads[q].wait()

    def own_pair(q, carry):
        transpose_pair(lambda i: raw[q, pl.ds(i, 2)], h, q + 2 - s, 1)
        return carry
    loop(4, own_pair)
    row_messages("x", "send")
    for copy in w1d_loads:
        copy.wait()

    def flat(value):
        return value.reshape(value.shape[0] * n, value.shape[-1])

    def dot(lhs, rhs):
        return jnp.dot(lhs, rhs, preferred_element_type=F32)

    def own_col(t, width):
        return jnp.where(is0, width - 1 - t, t)

    def phase(width, nch, item):
        def body(at, carry):
            item(lax.div(at, nch) - 1, lax.rem(at, nch))
            return carry
        lax.fori_loop((t_first + 1) * nch, (width + 1) * nch, body, 0)

    def y1_item(t, i):
        c = jnp.where(t < 3, lax.rem(i + 1, NCH), i)
        k = own_col(t, 4)

        @pl.when((t == t_first) & (i == NCH - 1))
        def _():
            row_messages("x", "recv")

        @pl.when((t == 3) & (lax.rem(i, NCH // 2) == 0))
        def _():
            half = lax.div(i, NCH // 2)
            for shift in SHIFTS:
                @pl.when(has_bwd & (s == shift))
                def _():
                    ref = xh.at[half, :, pl.ds(c0, c0)] if shift == 0 else xh.at[half]
                    remote(ref, ref, x_sem.at[half], x_sem.at[2 + half], row, bwd_col).wait_recv()
            transpose_pair(lambda j: xh[half, pl.ds(j, 2)], hh, jnp.where(is0, 1, 5), 1 + half * (h4 // 2))

        at = 1 + c * ch
        taps = []
        for kh in range(5):
            first, sub = (at - 1, 3) if kh == 0 else (at, kh - 1)
            for side in (1, 2):
                taps.append(flat(xs[k + side, pl.ds(first, ch), sub]))
        acc = dot(jnp.concatenate(taps, axis=1), w1d[...])
        void = last_void & (t == 3)
        for p in range(2):
            val = jnp.maximum(acc[:, p * c1:(p + 1) * c1] + b1d[...], 0.0)
            val = jnp.where(void, 0.0, val)
            y1[k + 2, pl.ds(at, ch), p] = val.astype(BF16).reshape(ch, n, c1)

        @pl.when((t == 0) & has_fwd)
        def _():
            y_copy(y1, PAIRS, ch, SEM_Y1, True, c, NCH).start()

        @pl.when((t == 3) & has_bwd)
        def _():
            y_copy(y1, PAIRS, ch, SEM_Y1, False, c, NCH).start()
    phase(PAIRS, NCH, y1_item)
    row_messages("y1", "send")
    for copy in w1c_loads:
        copy.wait()

    def wait_halo(ref, width, rows_per, sem0, forward, c, nch):
        exists = has_bwd if forward else has_fwd

        @pl.when(exists & (c == 0))
        def _():
            y_recv(ref, width, rows_per, sem0, forward, 0, nch).wait_recv()

        @pl.when(exists & (c < nch - 1))
        def _():
            y_recv(ref, width, rows_per, sem0, forward, c + 1, nch).wait_recv()

    def z1_item(o, i):
        t = jnp.where(o < 0, o, jnp.where(o == 3, o, lax.rem(o + 1, 3)))
        mid = jnp.where(i < NCH - 2, i + 1, jnp.where(i == NCH - 2, 0, NCH - 1))
        c = jnp.where(o < 2, mid, i)
        k = own_col(t, 4)

        @pl.when((o == t_first) & (i == NCH - 2))
        def _():
            row_messages("y1", "recv")

        @pl.when(t == 0)
        def _():
            wait_halo(y1, PAIRS, ch, SEM_Y1, False, c, NCH)

        @pl.when(t == 3)
        def _():
            wait_halo(y1, PAIRS, ch, SEM_Y1, True, c, NCH)

        at = 1 + c * ch
        taps = []
        for first, sub in ((at - 1, 1), (at, 0), (at, 1), (at + 1, 0)):
            for side in (1, 2, 3):
                taps.append(flat(y1[k + side, pl.ds(first, ch), sub]))
        for sub in (0, 2):
            taps.append(flat(xs[k + 2, pl.ds(at, ch), sub]))
        acc = dot(jnp.concatenate(taps, axis=1), w1c[...])
        for p in range(2):
            val = jnp.maximum(acc[:, p * c1:(p + 1) * c1] + b1c[...], 0.0)
            z1[k + 3 - s, pl.ds(at, ch), p] = val.astype(BF16).reshape(ch, n, c1)

        @pl.when((t == 0) & has_fwd)
        def _():
            z_copy(z1, PAIRS, ch, SEM_Z1, c).start()
    phase(PAIRS, NCH, z1_item)
    row_messages("z1", "send")
    for copy in w2d_loads + w3d_loads:
        copy.wait()

    def turn_weight(i, carry):
        turned = lax.dot_general(eye[0:c2, 0:c2], w3r[i], NT, preferred_element_type=F32)
        w3d[i] = turned.astype(BF16)
        return carry
    loop(9, turn_weight)
    wp3[...] = lax.dot_general(eye[0:c2, 0:c2], wp3r[...], NT, preferred_element_type=F32).astype(BF16)

    def y2_item(t, i):
        c = jnp.where(t < 1, lax.rem(i + 1, NCH), i)
        k = own_col(t, 2)

        @pl.when((t == t_first) & (i == NCH - 1))
        def _():
            row_messages("z1", "recv")

        @pl.when((t == 1) & has_bwd)
        def _():
            z_recv(z1, PAIRS, ch, SEM_Z1, c).wait_recv()

        at = 1 + c * ch
        taps = []
        for first, sub in ((at - 1, 1), (at, 0), (at, 1)):
            for side in range(3):
                taps.append(flat(z1[2 * k + 2 + side, pl.ds(first, ch), sub]))
        acc = dot(jnp.concatenate(taps, axis=1), w2d[...])
        val = jnp.maximum(acc + b2d[...], 0.0)
        val = jnp.where(last_void & (t == 1), 0.0, val)
        y2[k + 2, pl.ds(at, ch)] = val.astype(BF16).reshape(ch, n, c2)

        @pl.when((t == 0) & has_fwd)
        def _():
            y_copy(y2, 2, ch, SEM_Y2, True, c, NCH).start()

        @pl.when((t == 1) & has_bwd)
        def _():
            y_copy(y2, 2, ch, SEM_Y2, False, c, NCH).start()
    phase(2, NCH, y2_item)
    row_messages("y2", "send")
    for copy in w2c_loads:
        copy.wait()

    def z2_item(t, c):
        k = own_col(t, 2)

        @pl.when((t == t_first) & (c == 0))
        def _():
            row_messages("y2", "recv")

        @pl.when(t == 0)
        def _():
            wait_halo(y2, 2, ch, SEM_Y2, False, c, NCH)

        @pl.when(t == 1)
        def _():
            wait_halo(y2, 2, ch, SEM_Y2, True, c, NCH)

        at = 1 + c * ch
        taps = []
        for first in (at - 1, at, at + 1):
            for side in (1, 2, 3):
                taps.append(flat(y2[k + side, pl.ds(first, ch)]))
        taps.append(flat(z1[2 * k + 3, pl.ds(at, ch), 0]))
        acc = dot(jnp.concatenate(taps, axis=1), w2c[...])
        val = jnp.maximum(acc + b2c[...], 0.0).astype(BF16).reshape(ch // 2, 2, n, c2)
        z2[k + 3 - s, pl.ds(1 + c * (ch // 2), ch // 2)] = val

        @pl.when((t == 0) & has_fwd)
        def _():
            z_copy(z2, 2, ch // 2, SEM_Z2, c).start()
    phase(2, NCH, z2_item)
    row_messages("z2", "send")

    def y3_item(t, c):
        k = t

        @pl.when((t == t_first) & (c == 0))
        def _():
            row_messages("z2", "recv")

        @pl.when((t == 0) & has_bwd)
        def _():
            for j in range(NCH // NCH3):
                z_recv(z2, 2, ch // 2, SEM_Z2, c * (NCH // NCH3) + j).wait_recv()

        at = 1 + c * ch3
        acc = jnp.zeros((ch3 * n, c3), F32)
        tap = 0
        for first, sub in ((at - 1, 1), (at, 0), (at, 1)):
            for side in range(3):
                acc = acc + dot(flat(z2[2 * k + 2 + side, pl.ds(first, ch3), sub]), w3d[tap])
                tap += 1
        val = jnp.maximum(acc + b3d[...], 0.0)
        val = jnp.where(last_void & (t == 0), 0.0, val)
        y3[k + 2, pl.ds(at, ch3)] = val.astype(BF16).reshape(ch3, n, c3)

        @pl.when((t == 0) & has_fwd)
        def _():
            y_copy(y3, 1, ch3, SEM_Y3, True, c, NCH3).start()

        @pl.when((t == 0) & has_bwd)
        def _():
            y_copy(y3, 1, ch3, SEM_Y3, False, c, NCH3).start()
    phase(1, NCH3, y3_item)
    row_messages("y3", "send")
    for copy in w3c_loads:
        copy.wait()

    ships = (s == 1) & has_bwd

    def ship(c):
        part = pl.ds(c * ch3, ch3)
        return remote(zo.at[1, part], out_hbm.at[part], out_sem.at[c], out_sem.at[NCH3 + c], row, bwd_col)

    def ship_recv(c):
        part = pl.ds(c * ch3, ch3)
        return remote(zo.at[1, part], out_hbm.at[part], out_sem.at[c], out_sem.at[NCH3 + c], row, fwd_col)

    keep = jnp.where(is0, 1, 0)

    def put(c):
        part = pl.ds(c * ch3, ch3)
        return pltpu.make_async_copy(zo.at[keep, part], out_hbm.at[part], out_sem.at[2 * NCH3 + c])

    def z3_item(t, c):
        k = t

        @pl.when((t == t_first) & (c == 0))
        def _():
            row_messages("y3", "recv")

        @pl.when(t == 0)
        def _():
            wait_halo(y3, 1, ch3, SEM_Y3, False, c, NCH3)
            wait_halo(y3, 1, ch3, SEM_Y3, True, c, NCH3)

        at = 1 + c * ch3
        acc = dot(flat(z2[2 * k + 3, pl.ds(at, ch3), 0]), wp3[...])
        tap = 0
        for first in (at - 1, at, at + 1):
            for side in (1, 2, 3):
                acc = acc + dot(flat(y3[k + side, pl.ds(first, ch3)]), w3c[tap])
                tap += 1
        val = jnp.maximum(acc + b3c[...], 0.0)
        zo[k + 1, pl.ds(c * ch3, ch3)] = val.astype(BF16).reshape(ch3, n, c3)

        @pl.when((t == 0) & ships)
        def _():
            ship(c).start()

        @pl.when(((t == 0) & is0) | (t == -1))
        def _():
            put(c).start()
    phase(1, NCH3, z3_item)

    for shift in SHIFTS:
        @pl.when(has_fwd & (s == shift))
        def _():
            for half in range(2):
                x_copy(shift, half).wait_send()

    def drain(c, carry):
        @pl.when(has_fwd)
        def _():
            y_copy(y1, PAIRS, ch, SEM_Y1, True, c, NCH).wait_send()
            z_copy(z1, PAIRS, ch, SEM_Z1, c).wait_send()
            y_copy(y2, 2, ch, SEM_Y2, True, c, NCH).wait_send()
            z_copy(z2, 2, ch // 2, SEM_Z2, c).wait_send()

        @pl.when(has_bwd)
        def _():
            y_copy(y1, PAIRS, ch, SEM_Y1, False, c, NCH).wait_send()
            y_copy(y2, 2, ch, SEM_Y2, False, c, NCH).wait_send()
        return carry
    loop(NCH, drain)

    def drain3(c, carry):
        @pl.when(has_fwd)
        def _():
            y_copy(y3, 1, ch3, SEM_Y3, True, c, NCH3).wait_send()

        @pl.when(has_bwd)
        def _():
            y_copy(y3, 1, ch3, SEM_Y3, False, c, NCH3).wait_send()

        @pl.when(ships)
        def _():
            ship(c).wait_send()

        @pl.when((s == 1) & has_fwd)
        def _():
            ship_recv(c).wait_recv()

        @pl.when(is0 | first_extra)
        def _():
            put(c).wait()
        return carry
    loop(NCH3, drain3)
    for name in ROW_SEM:
        row_messages(name, "sent")


def solution(mesh):
    rows = mesh.shape["row"]
    cols = mesh.shape["col"]
    tile_spec = P("batch", "row", "col")

    def local_blocks(x, w1d, b1d, w1c, b1c, wp1, w2d, b2d, w2c, b2c, wp2, w3d, b3d, w3c, b3c, wp3):
        n, h, w, c0 = x.shape
        c1, c2, c3 = w1d.shape[3], w2d.shape[3], w3d.shape[3]
        h4, h8 = h // 4, h // 8
        dims = (n, h, c0, c1, c2, c3, rows, cols)
        pair = 2 * c0
        xt = jnp.moveaxis(x, 1, 3).reshape(n, PAIRS, pair, h)
        args = (xt, w1d.reshape(3, 3 * c0, c1), w1c.reshape(9 * c1, c1), wp1, w2d.reshape(9 * c1, c2), w2c.reshape(9 * c2, c2), wp2,
                jnp.swapaxes(w3d.reshape(9, c2, c3), 1, 2), w3c.reshape(9, c3, c3), wp3.T,
                *(bias.reshape(1, -1) for bias in (b1d, b1c, b2d, b2c, b3d, b3c)))
        vm = pltpu.VMEM
        dma = pltpu.SemaphoreType.DMA
        flops = 2 * n * h * w * c1 * 7 * (c0 + c1)
        out = pl.pallas_call(
            functools.partial(kernel, dims),
            out_shape=jax.ShapeDtypeStruct((h8, n, c3), BF16),
            in_specs=[pl.BlockSpec(memory_space=pl.ANY)] * len(args),
            out_specs=pl.BlockSpec(memory_space=pl.ANY),
            scratch_shapes=[
                vm((PAIRS, n, pair, h), BF16), vm((2, n, pair, h // 2), BF16), vm((h * n, pair), F32), vm((h, h), BF16),
                vm((6, h4 + 1, 4, n, pair), BF16), vm((7, h4 + 2, 2, n, c1), BF16), vm((7, h4 + 1, 2, n, c1), BF16),
                vm((5, h4 + 2, n, c2), BF16), vm((5, h8 + 1, 2, n, c2), BF16), vm((4, h8 + 2, n, c3), BF16), vm((2, h8, n, c3), BF16),
                vm((10 * pair, 2 * c1), BF16), vm((12 * c1 + 2 * pair, 2 * c1), BF16), vm((9 * c1, c2), BF16), vm((9 * c2 + c1, c2), BF16),
                vm((9, c3, c2), BF16), vm((9, c2, c3), BF16), vm((9, c3, c3), BF16), vm((c3, c2), BF16), vm((c2, c3), BF16),
            ] + [vm((1, width), F32) for width in (c1, c1, c2, c2, c3, c3)] + [
                dma((count,)) for count in (32, 4, 10 * NCH, 10 * NCH, 12 * MAX_PLAN, 12 * MAX_PLAN, 3 * NCH3)],
            compiler_params=pltpu.CompilerParams(collective_id=0, has_side_effects=True, vmem_limit_bytes=63 * 1024 * 1024),
            cost_estimate=pl.CostEstimate(flops=flops, bytes_accessed=16 * 1024 * 1024, transcendentals=0),
        )(*args)
        return jnp.swapaxes(out, 0, 1).reshape(n, h8, 1, c3)

    return jax.shard_map(local_blocks, mesh=mesh, in_specs=(tile_spec,) + (P(),) * 15, out_specs=tile_spec, check_vma=False)
```

time: 226 us -> 92.5 us (0.41)
  the two profiles are of different devices: /device:TPU:1 before, /device:TPU:13 now
where the time goes in v1:
time: 92.5 us; the launch traced here: 91.1 us
  Pallas kernels  86.8 us (94%)
  local copies, waits for them, and re-layouts  4.32 us (5%)
    pallas_call x1, Pallas kernels, local_blocks(): pl.pallas_call(functools.partial(kernel, dims), out_shape=jax.ShapeDtypeS...  86.8 us
    reshape x2, local copies, waits for them, and re-layouts, local_blocks(): bias.reshape(1, -1)  2.5 us

profile of v1, /device:TPU:13, one launch (start us, length us, event | category | flops | bytes accessed | tf_op | source)
XLA Modules:
  0.0 91.1 jit_solution(5938492972518712169)
XLA Ops:
  0.0 1.2 %reshape.53.b3d_h = f32[1,320]{1,0:T(1,128)} reshape(f32[320]{0:T(512)} %param.28) | data formatting | bytes 2560 | tf_op jit(solution)/shard_map/reshape | solution.py:594
  1.2 1.3 %reshape.54.b3c_h = f32[1,320]{1,0:T(1,128)} reshape(f32[320]{0:T(512)} %param.30) | data formatting | bytes 2560 | tf_op jit(solution)/shard_map/reshape | solution.py:594
  2.5 86.8 %shard_map.154 = bf16[32,16,320]{2,1,0:T(8,128)(2,1)} custom-call(bf16[16,4,128,256]{3,2,1,0:T(8,128)(2,1)} %bitcast.20, bf16[3,192,128]{2,1,0:T(8,128)(2,1)} %bitcast.27, bf16[1152,128]{1,0:T(8,128)(2,1)} %bitcast.25, bf16[64,128]{1,0:T(8,128)(2,1)} %wp1_h.1, bf16[1152,256]{1,0:T(8,128)(2,1)} %bitcast.24, bf16[2304,256]{1,0:T(8,128)(2,1)} %bitcast.23, ...), custom_call_target="tpu_custom_call" | custom-call | flops 11274289152 | bytes 16777216 | tf_op jit(solution)/shard_map/pallas_call | solution.py:598
  89.3 1.8 %copy.17 = bf16[16,32,1,320]{3,1,2,0:T(8,128)(2,1)} copy(bf16[16,32,1,320]{3,0,1,2:T(8,128)(2,1)} %bitcast.19) | data formatting | bytes 655360 | tf_op jit(solution)/shard_map/reshape | solution.py:614

commit v2 on v1

--- a/solution.py
+++ b/solution.py
@@ -14,6 +14,8 @@
 NCH3 = 2
 PAIRS = 4
 MAX_PLAN = 5
+BLOCK = 16
+UNROLL = 4
 OWN, HALO = range(2)
 NT = (((1,), (1,)), ((), ()))
 
@@ -47,7 +49,7 @@
 
 
 def kernel(dims, x_hbm, w1d_h, w1c_h, wp1_h, w2d_h, w2c_h, wp2_h, w3d_h, w3c_h, wp3_h, b1d_h, b1c_h, b2d_h, b2c_h, b3d_h, b3c_h, out_hbm,
-           raw, xh, stage_f, eye, xs, y1, z1, y2, z2, y3, zo, w1d, w1c, w2d, w2c, w3r, w3d, w3c, wp3r, wp3,
+           raw, xh, turned, eye, mix, xs, y1, z1, y2, z2, y3, zo, w1d, w1c, w2d, w2c, w3r, w3d, w3c, wp3r, wp3,
            b1d, b1c, b2d, b2c, b3d, b3c, load_sem, x_sem, col_send, col_recv, row_send, row_recv, out_sem):
     n, h, c0, c1, c2, c3, rows, cols = dims
     h4, h8 = h // 4, h // 8
@@ -74,7 +76,7 @@
     k1, k2 = 9 * c1, 9 * c2
     pair = 2 * c0
     x_loads = [load(x_hbm.at[:, q], raw.at[q]) for q in range(PAIRS)]
-    w1d_loads = [load(b1d_h, b1d), load(b1c_h, b1c)]
+    w1d_loads = [load(b1d_h, b1d.at[0]), load(b1c_h, b1c.at[0])]
     w1c_loads = []
     for p in range(2):
         lanes = pl.ds(p * c1, c1)
@@ -82,10 +84,10 @@
             w1d_loads.append(load(w1d_h.at[kh], w1d.at[pl.ds((kh + 2 * p) * 2 * pair + c0, 3 * c0), lanes]))
         w1c_loads.append(load(w1c_h, w1c.at[pl.ds(p * 3 * c1, k1), lanes]))
         w1c_loads.append(load(wp1_h, w1c.at[pl.ds(12 * c1 + p * pair, c0), lanes]))
-    w2d_loads = [load(w2d_h, w2d), load(b2d_h, b2d)]
-    w2c_loads = [load(w2c_h, w2c.at[pl.ds(0, k2)]), load(wp2_h, w2c.at[pl.ds(k2, c1)]), load(b2c_h, b2c)]
-    w3d_loads = [load(w3d_h, w3r), load(b3d_h, b3d), load(wp3_h, wp3r)]
-    w3c_loads = [load(w3c_h, w3c), load(b3c_h, b3c)]
+    w2d_loads = [load(w2d_h, w2d), load(b2d_h, b2d.at[0])]
+    w2c_loads = [load(w2c_h, w2c.at[pl.ds(0, k2)]), load(wp2_h, w2c.at[pl.ds(k2, c1)]), load(b2c_h, b2c.at[0])]
+    w3d_loads = [load(w3d_h, w3r), load(b3d_h, b3d.at[0]), load(wp3_h, wp3r)]
+    w3c_loads = [load(w3c_h, w3c), load(b3c_h, b3c.at[0])]
     for copy in x_loads + w1d_loads + w1c_loads + w2d_loads + w2c_loads + w3d_loads + w3c_loads:
         copy.start()
 
@@ -106,6 +108,9 @@
 
     def directions(name):
         return (True, False) if ROW_SEM[name][0] == "y" else (True,)
+
+    def dot(lhs, rhs):
+        return jnp.dot(lhs, rhs, preferred_element_type=F32)
 
     def zero_slot(ref, idx):
         def body(i, carry):
@@ -223,25 +228,57 @@
                             else:
                                 copy.wait_send()
 
-    eye[...] = (lax.broadcasted_iota(jnp.int32, (h, h), 0) == lax.broadcasted_iota(jnp.int32, (h, h), 1)).astype(F32).astype(BF16)
-
-    def transpose_pair(read, size, slot, h4_first):
-        unit = eye[0:size, 0:size]
-
+    def unit_where(size, source):
+        at = lax.broadcasted_iota(jnp.int32, (size, size), 0)
+        return (at == source(lax.broadcasted_iota(jnp.int32, (size, size), 1))).astype(F32).astype(BF16)
+
+    eye[...] = unit_where(h, lambda at: at)
+    mix[...] = unit_where(n * BLOCK, lambda at: (at & (BLOCK - 1)) * n + (at >> BLOCK.bit_length() - 1))
+
+    def to_rows(value):
+        return value.astype(BF16).reshape(BLOCK // 4, 4, n, pair)
+
+    def turn_group(q):
         def turn(i, carry):
-            block = read(2 * i).reshape(2 * pair, size)
-            turned = lax.dot_general(unit, block, NT, preferred_element_type=F32)
+            for j in range(UNROLL):
+                at = i * UNROLL + j
+                block = raw[pl.ds(q, 2), at].reshape(2 * pair, h)
+                turned[at] = lax.dot_general(eye[...], block, NT, preferred_element_type=F32).astype(BF16)
+            return carry
+        loop(n // UNROLL, turn)
+
+        def place(i, carry):
+            for j in range(UNROLL):
+                at = i * UNROLL + j
+                block = turned[:, pl.ds(at * BLOCK, BLOCK), :].reshape(n * BLOCK, 2 * pair)
+                moved = dot(mix[...], block)
+                for side in range(2):
+                    xs[q + 2 - s + side, pl.ds(1 + at * (BLOCK // 4), BLOCK // 4)] = to_rows(moved[:, side * pair:(side + 1) * pair])
+            return carry
+        loop(h // BLOCK // UNROLL, place)
+
+    def turn_halo(half):
+        slot = jnp.where(is0, 1, PAIRS + 1)
+        unit = eye[:hh, :hh]
+
+        def turn(i, carry):
+            for j in range(UNROLL):
+                at = 2 * (i * UNROLL + j)
+                block = xh[half, pl.ds(at, 2)].reshape(2 * pair, hh)
+                both = lax.dot_general(unit, block, NT, preferred_element_type=F32).astype(BF16)
+                for side in range(2):
+                    turned[at + side, :hh, :pair] = both[:, side * pair:(side + 1) * pair]
+            return carry
+        loop(n // 2 // UNROLL, turn)
+
+        def place(i, carry):
+            blocks = [turned[:, pl.ds((2 * i + j) * BLOCK, BLOCK), :pair].reshape(n * BLOCK, pair) for j in range(2)]
+            moved = dot(mix[...], jnp.concatenate(blocks, axis=1))
             for j in range(2):
-                stage_f[pl.ds(2 * i + j, size, stride=n), :] = turned[:, j * pair:(j + 1) * pair]
+                first = 1 + half * (h4 // 2) + (2 * i + j) * (BLOCK // 4)
+                xs[slot, pl.ds(first, BLOCK // 4)] = to_rows(moved[:, j * pair:(j + 1) * pair])
             return carry
-        loop(n // 2, turn)
-        step = 4
-
-        def pack(i, carry):
-            part = stage_f[pl.ds(i * (step * 4 * n), step * 4 * n), :]
-            xs[slot, pl.ds(h4_first + i * step, step)] = part.reshape(step, 4, n, 2 * c0).astype(BF16)
-            return carry
-        loop(size // 4 // step, pack)
+        loop(hh // BLOCK // 2, place)
 
     def zero_part(ref, first, size, p):
         ref[pl.ds(first, size), pl.ds(p * c1, c1)] = jnp.zeros((size, c1), BF16)
@@ -258,22 +295,11 @@
             zero_part(w1c, proj_at + p * pair + c0, c0, p)
 
     zero_weights()
-    for q in range(4):
-        x_loads[q].wait()
-
-    def own_pair(q, carry):
-        transpose_pair(lambda i: raw[q, pl.ds(i, 2)], h, q + 2 - s, 1)
-        return carry
-    loop(4, own_pair)
-    row_messages("x", "send")
-    for copy in w1d_loads:
+    for copy in x_loads + w1d_loads:
         copy.wait()
 
     def flat(value):
         return value.reshape(value.shape[0] * n, value.shape[-1])
-
-    def dot(lhs, rhs):
-        return jnp.dot(lhs, rhs, preferred_element_type=F32)
 
     def own_col(t, width):
         return jnp.where(is0, width - 1 - t, t)
@@ -284,23 +310,34 @@
             return carry
         lax.fori_loop((t_first + 1) * nch, (width + 1) * nch, body, 0)
 
-    def y1_item(t, i):
-        c = jnp.where(t < 3, lax.rem(i + 1, NCH), i)
-        k = own_col(t, 4)
-
-        @pl.when((t == t_first) & (i == NCH - 1))
+    def y1_item(at, carry):
+        early = 3 - t_first
+        t = jnp.where(at < 3 * early, lax.div(at, 3) + t_first, at - 3 * early + t_first)
+        t = jnp.where(at < NCH * early, t, 3)
+        c = jnp.where(at < 3 * early, lax.rem(at, 3) + 1, jnp.where(t < 3, 0, at - NCH * early))
+        k = own_col(t, PAIRS)
+
+        @pl.when((at == 0) | (t == 1) & (c == 1))
+        def _():
+            turn_group(2 * jnp.where(is0 == (t < 1), 1, 0))
+
+        @pl.when((t == 1) & (c == 1))
+        def _():
+            row_messages("x", "send")
+
+        @pl.when(at == 3 * early)
         def _():
             row_messages("x", "recv")
 
-        @pl.when((t == 3) & (lax.rem(i, NCH // 2) == 0))
-        def _():
-            half = lax.div(i, NCH // 2)
+        @pl.when((t == 3) & (lax.rem(c, NCH // 2) == 0))
+        def _():
+            half = lax.div(c, NCH // 2)
             for shift in SHIFTS:
                 @pl.when(has_bwd & (s == shift))
                 def _():
                     ref = xh.at[half, :, pl.ds(c0, c0)] if shift == 0 else xh.at[half]
                     remote(ref, ref, x_sem.at[half], x_sem.at[2 + half], row, bwd_col).wait_recv()
-            transpose_pair(lambda j: xh[half, pl.ds(j, 2)], hh, jnp.where(is0, 1, 5), 1 + half * (h4 // 2))
+            turn_halo(half)
 
         at = 1 + c * ch
         taps = []
@@ -322,7 +359,8 @@
         @pl.when((t == 3) & has_bwd)
         def _():
             y_copy(y1, PAIRS, ch, SEM_Y1, False, c, NCH).start()
-    phase(PAIRS, NCH, y1_item)
+        return carry
+    lax.fori_loop(0, NCH * (PAIRS - t_first), y1_item, 0)
     row_messages("y1", "send")
     for copy in w1c_loads:
         copy.wait()
@@ -591,7 +629,7 @@
         xt = jnp.moveaxis(x, 1, 3).reshape(n, PAIRS, pair, h)
         args = (xt, w1d.reshape(3, 3 * c0, c1), w1c.reshape(9 * c1, c1), wp1, w2d.reshape(9 * c1, c2), w2c.reshape(9 * c2, c2), wp2,
                 jnp.swapaxes(w3d.reshape(9, c2, c3), 1, 2), w3c.reshape(9, c3, c3), wp3.T,
-                *(bias.reshape(1, -1) for bias in (b1d, b1c, b2d, b2c, b3d, b3c)))
+                b1d, b1c, b2d, b2c, b3d, b3c)
         vm = pltpu.VMEM
         dma = pltpu.SemaphoreType.DMA
         flops = 2 * n * h * w * c1 * 7 * (c0 + c1)
@@ -601,7 +639,7 @@
             in_specs=[pl.BlockSpec(memory_space=pl.ANY)] * len(args),
             out_specs=pl.BlockSpec(memory_space=pl.ANY),
             scratch_shapes=[
-                vm((PAIRS, n, pair, h), BF16), vm((2, n, pair, h // 2), BF16), vm((h * n, pair), F32), vm((h, h), BF16),
+                vm((PAIRS, n, pair, h), BF16), vm((2, n, pair, h // 2), BF16), vm((n, h, 2 * pair), BF16), vm((h, h), BF16), vm((n * BLOCK, n * BLOCK), BF16),
                 vm((6, h4 + 1, 4, n, pair), BF16), vm((7, h4 + 2, 2, n, c1), BF16), vm((7, h4 + 1, 2, n, c1), BF16),
                 vm((5, h4 + 2, n, c2), BF16), vm((5, h8 + 1, 2, n, c2), BF16), vm((4, h8 + 2, n, c3), BF16), vm((2, h8, n, c3), BF16),
                 vm((10 * pair, 2 * c1), BF16), vm((12 * c1 + 2 * pair, 2 * c1), BF16), vm((9 * c1, c2), BF16), vm((9 * c2 + c1, c2), BF16),

time: 92.5 us -> 88.1 us (0.952)
  local copies, waits for them, and re-layouts: 4.32 us -> 1.82 us
  Pallas kernels: 86.8 us -> 85 us
    reshape x2 -> x0, local copies, waits for them, and re-layouts: 2.5 us -> none  [local_blocks(): bias.reshape(1, -1)]
    pallas_call x1, Pallas kernels: 86.8 us -> 85 us  [local_blocks(): pl.pallas_call(functools.partial(kernel, dims), out_shape=jax.ShapeDtypeS...]
where the time goes in v2:
time: 88.1 us; the launch traced here: 86.8 us
  Pallas kernels  85 us (96%)
  local copies, waits for them, and re-layouts  1.82 us (2%)
    pallas_call x1, Pallas kernels, local_blocks(): pl.pallas_call(functools.partial(kernel, dims), out_shape=jax.ShapeDtypeS...  85 us
    reshape x1, local copies, waits for them, and re-layouts, local_blocks(): return jnp.swapaxes(out, 0, 1).reshape(n, h8, 1, c3)  1.82 us

profile of v2, /device:TPU:13, one launch (start us, length us, event | category | flops | bytes accessed | tf_op | source)
XLA Modules:
  0.0 86.8 jit_solution(9303435580422551649)
XLA Ops:
  0.0 85.0 %shard_map.154 = bf16[32,16,320]{2,1,0:T(8,128)(2,1)} custom-call(bf16[16,4,128,256]{3,2,1,0:T(8,128)(2,1)} %bitcast.16, bf16[3,192,128]{2,1,0:T(8,128)(2,1)} %bitcast.23, bf16[1152,128]{1,0:T(8,128)(2,1)} %bitcast.21, bf16[64,128]{1,0:T(8,128)(2,1)} %wp1_h.1, bf16[1152,256]{1,0:T(8,128)(2,1)} %bitcast.20, bf16[2304,256]{1,0:T(8,128)(2,1)} %bitcast.19, ...), custom_call_target="tpu_custom_call" | custom-call | flops 11274289152 | bytes 16777216 | tf_op jit(solution)/shard_map/pallas_call | solution.py:636
  85.0 1.8 %copy.17 = bf16[16,32,1,320]{3,1,2,0:T(8,128)(2,1)} copy(bf16[16,32,1,320]{3,0,1,2:T(8,128)(2,1)} %bitcast.15) | data formatting | bytes 655360 | tf_op jit(solution)/shard_map/reshape | solution.py:652

commit v3 on v2

--- a/solution.py
+++ b/solution.py
@@ -18,6 +18,10 @@
 UNROLL = 4
 OWN, HALO = range(2)
 NT = (((1,), (1,)), ((), ()))
+
+
+def relu(value):
+    return jnp.maximum(value, 0.0)
 
 
 def loop(count, body):
@@ -49,7 +53,7 @@
 
 
 def kernel(dims, x_hbm, w1d_h, w1c_h, wp1_h, w2d_h, w2c_h, wp2_h, w3d_h, w3c_h, wp3_h, b1d_h, b1c_h, b2d_h, b2c_h, b3d_h, b3c_h, out_hbm,
-           raw, xh, turned, eye, mix, xs, y1, z1, y2, z2, y3, zo, w1d, w1c, w2d, w2c, w3r, w3d, w3c, wp3r, wp3,
+           raw, xh, turned, eye, mix, xs, y1, z1, y2, z2, y3, zo, w1d, w1c, w2d, w2c, w3r, w3c, wp3r,
            b1d, b1c, b2d, b2c, b3d, b3c, load_sem, x_sem, col_send, col_recv, row_send, row_recv, out_sem):
     n, h, c0, c1, c2, c3, rows, cols = dims
     h4, h8 = h // 4, h // 8
@@ -301,6 +305,13 @@
     def flat(value):
         return value.reshape(value.shape[0] * n, value.shape[-1])
 
+    def parts(first, count):
+        size = count // 2
+        return tuple((first + i * size, size) for i in range(2))
+
+    def dot_nt(lhs, rhs):
+        return lax.dot_general(lhs, rhs, NT, preferred_element_type=F32)
+
     def own_col(t, width):
         return jnp.where(is0, width - 1 - t, t)
 
@@ -310,35 +321,8 @@
             return carry
         lax.fori_loop((t_first + 1) * nch, (width + 1) * nch, body, 0)
 
-    def y1_item(at, carry):
-        early = 3 - t_first
-        t = jnp.where(at < 3 * early, lax.div(at, 3) + t_first, at - 3 * early + t_first)
-        t = jnp.where(at < NCH * early, t, 3)
-        c = jnp.where(at < 3 * early, lax.rem(at, 3) + 1, jnp.where(t < 3, 0, at - NCH * early))
+    def y1_job(t, c):
         k = own_col(t, PAIRS)
-
-        @pl.when((at == 0) | (t == 1) & (c == 1))
-        def _():
-            turn_group(2 * jnp.where(is0 == (t < 1), 1, 0))
-
-        @pl.when((t == 1) & (c == 1))
-        def _():
-            row_messages("x", "send")
-
-        @pl.when(at == 3 * early)
-        def _():
-            row_messages("x", "recv")
-
-        @pl.when((t == 3) & (lax.rem(c, NCH // 2) == 0))
-        def _():
-            half = lax.div(c, NCH // 2)
-            for shift in SHIFTS:
-                @pl.when(has_bwd & (s == shift))
-                def _():
-                    ref = xh.at[half, :, pl.ds(c0, c0)] if shift == 0 else xh.at[half]
-                    remote(ref, ref, x_sem.at[half], x_sem.at[2 + half], row, bwd_col).wait_recv()
-            turn_halo(half)
-
         at = 1 + c * ch
         taps = []
         for kh in range(5):
@@ -348,19 +332,51 @@
         acc = dot(jnp.concatenate(taps, axis=1), w1d[...])
         void = last_void & (t == 3)
         for p in range(2):
-            val = jnp.maximum(acc[:, p * c1:(p + 1) * c1] + b1d[...], 0.0)
+            val = relu(acc[:, p * c1:(p + 1) * c1] + b1d[...])
             val = jnp.where(void, 0.0, val)
             y1[k + 2, pl.ds(at, ch), p] = val.astype(BF16).reshape(ch, n, c1)
 
-        @pl.when((t == 0) & has_fwd)
-        def _():
-            y_copy(y1, PAIRS, ch, SEM_Y1, True, c, NCH).start()
-
-        @pl.when((t == 3) & has_bwd)
-        def _():
-            y_copy(y1, PAIRS, ch, SEM_Y1, False, c, NCH).start()
-        return carry
-    lax.fori_loop(0, NCH * (PAIRS - t_first), y1_item, 0)
+    def own_group(group, carry):
+        turn_group(2 * group)
+        return carry
+    loop(PAIRS // 2, own_group)
+    row_messages("x", "send")
+    early = 3 - t_first
+
+    def y1_item(item, carry):
+        @pl.when(item == lax.div(3 * early, 2))
+        def _():
+            row_messages("x", "recv")
+
+        half = item - 2 * early
+
+        @pl.when(half >= 0)
+        def _():
+            for shift in SHIFTS:
+                @pl.when(has_bwd & (s == shift))
+                def _():
+                    ref = xh.at[half, :, pl.ds(c0, c0)] if shift == 0 else xh.at[half]
+                    remote(ref, ref, x_sem.at[half], x_sem.at[2 + half], row, bwd_col).wait_recv()
+            turn_halo(half)
+
+        jobs = []
+        for j in range(2):
+            at = 2 * item + j
+            t = jnp.where(at < 3 * early, lax.div(at, 3) + t_first, jnp.where(half >= 0, 3, at - 3 * early + t_first))
+            c = jnp.where(at < 3 * early, lax.rem(at, 3) + 1, jnp.where(half >= 0, at - NCH * early, 0))
+            jobs.append((t, c))
+        for t, c in jobs:
+            y1_job(t, c)
+        for t, c in jobs:
+            @pl.when((t == 0) & has_fwd)
+            def _():
+                y_copy(y1, PAIRS, ch, SEM_Y1, True, c, NCH).start()
+
+            @pl.when((t == 3) & has_bwd)
+            def _():
+                y_copy(y1, PAIRS, ch, SEM_Y1, False, c, NCH).start()
+        return carry
+    loop(2 * (PAIRS - t_first), y1_item)
     row_messages("y1", "send")
     for copy in w1c_loads:
         copy.wait()
@@ -376,24 +392,8 @@
         def _():
             y_recv(ref, width, rows_per, sem0, forward, c + 1, nch).wait_recv()
 
-    def z1_item(o, i):
-        t = jnp.where(o < 0, o, jnp.where(o == 3, o, lax.rem(o + 1, 3)))
-        mid = jnp.where(i < NCH - 2, i + 1, jnp.where(i == NCH - 2, 0, NCH - 1))
-        c = jnp.where(o < 2, mid, i)
-        k = own_col(t, 4)
-
-        @pl.when((o == t_first) & (i == NCH - 2))
-        def _():
-            row_messages("y1", "recv")
-
-        @pl.when(t == 0)
-        def _():
-            wait_halo(y1, PAIRS, ch, SEM_Y1, False, c, NCH)
-
-        @pl.when(t == 3)
-        def _():
-            wait_halo(y1, PAIRS, ch, SEM_Y1, True, c, NCH)
-
+    def z1_job(t, c):
+        k = own_col(t, PAIRS)
         at = 1 + c * ch
         taps = []
         for first, sub in ((at - 1, 1), (at, 0), (at, 1), (at + 1, 0)):
@@ -403,73 +403,89 @@
             taps.append(flat(xs[k + 2, pl.ds(at, ch), sub]))
         acc = dot(jnp.concatenate(taps, axis=1), w1c[...])
         for p in range(2):
-            val = jnp.maximum(acc[:, p * c1:(p + 1) * c1] + b1c[...], 0.0)
+            val = relu(acc[:, p * c1:(p + 1) * c1] + b1c[...])
             z1[k + 3 - s, pl.ds(at, ch), p] = val.astype(BF16).reshape(ch, n, c1)
 
-        @pl.when((t == 0) & has_fwd)
-        def _():
-            z_copy(z1, PAIRS, ch, SEM_Z1, c).start()
-    phase(PAIRS, NCH, z1_item)
+    extra = -t_first
+
+    def z1_item(item, carry):
+        inner = item - extra
+        edge = inner - NCH - extra
+        more = (inner < 0) | (extra == 1) & (inner == NCH)
+
+        @pl.when(inner == 2)
+        def _():
+            row_messages("y1", "recv")
+
+        @pl.when(edge >= 0)
+        def _():
+            wait_halo(y1, PAIRS, ch, SEM_Y1, False, edge, NCH)
+            wait_halo(y1, PAIRS, ch, SEM_Y1, True, edge, NCH)
+
+        mid = jnp.where(inner < 2, inner + 1, jnp.where(inner == 2, 0, inner))
+        for j in range(2):
+            t = jnp.where(more, -1, jnp.where(edge >= 0, 3 * j, j + 1))
+            c = jnp.where(more, jnp.where(inner < 0, j + 1, 3 * j), jnp.where(edge >= 0, edge, mid))
+            z1_job(t, c)
+
+        @pl.when((edge >= 0) & has_fwd)
+        def _():
+            z_copy(z1, PAIRS, ch, SEM_Z1, edge).start()
+        return carry
+    loop(2 * (NCH + extra), z1_item)
     row_messages("z1", "send")
-    for copy in w2d_loads + w3d_loads:
+    for copy in w2d_loads:
         copy.wait()
 
-    def turn_weight(i, carry):
-        turned = lax.dot_general(eye[0:c2, 0:c2], w3r[i], NT, preferred_element_type=F32)
-        w3d[i] = turned.astype(BF16)
-        return carry
-    loop(9, turn_weight)
-    wp3[...] = lax.dot_general(eye[0:c2, 0:c2], wp3r[...], NT, preferred_element_type=F32).astype(BF16)
-
-    def y2_item(t, i):
-        c = jnp.where(t < 1, lax.rem(i + 1, NCH), i)
+    def y2_job(t, at, size):
         k = own_col(t, 2)
-
-        @pl.when((t == t_first) & (i == NCH - 1))
-        def _():
-            row_messages("z1", "recv")
-
-        @pl.when((t == 1) & has_bwd)
-        def _():
-            z_recv(z1, PAIRS, ch, SEM_Z1, c).wait_recv()
-
-        at = 1 + c * ch
         taps = []
         for first, sub in ((at - 1, 1), (at, 0), (at, 1)):
             for side in range(3):
-                taps.append(flat(z1[2 * k + 2 + side, pl.ds(first, ch), sub]))
+                taps.append(flat(z1[2 * k + 2 + side, pl.ds(first, size), sub]))
         acc = dot(jnp.concatenate(taps, axis=1), w2d[...])
-        val = jnp.maximum(acc + b2d[...], 0.0)
+        val = relu(acc + b2d[...])
         val = jnp.where(last_void & (t == 1), 0.0, val)
-        y2[k + 2, pl.ds(at, ch)] = val.astype(BF16).reshape(ch, n, c2)
+        y2[k + 2, pl.ds(at, size)] = val.astype(BF16).reshape(size, n, c2)
+
+    def y2_inner(item, carry):
+        t = t_first + lax.div(item, 2)
+        late = lax.rem(item, 2)
+
+        @pl.when(item == 1)
+        def _():
+            row_messages("z1", "recv")
+
+        chunks = (1 + 2 * late, 2 - 2 * late)
+        for c in chunks:
+            y2_job(t, 1 + c * ch, ch)
 
         @pl.when((t == 0) & has_fwd)
         def _():
-            y_copy(y2, 2, ch, SEM_Y2, True, c, NCH).start()
-
-        @pl.when((t == 1) & has_bwd)
+            for c in chunks:
+                y_copy(y2, 2, ch, SEM_Y2, True, c, NCH).start()
+        return carry
+    loop(2 + 2 * extra, y2_inner)
+
+    def y2_edge(c, carry):
+        @pl.when(has_bwd)
+        def _():
+            z_recv(z1, PAIRS, ch, SEM_Z1, c).wait_recv()
+
+        for at, size in parts(1 + c * ch, ch):
+            y2_job(jnp.int32(1), at, size)
+
+        @pl.when(has_bwd)
         def _():
             y_copy(y2, 2, ch, SEM_Y2, False, c, NCH).start()
-    phase(2, NCH, y2_item)
+        return carry
+    loop(NCH, y2_edge)
     row_messages("y2", "send")
     for copy in w2c_loads:
         copy.wait()
 
-    def z2_item(t, c):
+    def z2_job(t, c):
         k = own_col(t, 2)
-
-        @pl.when((t == t_first) & (c == 0))
-        def _():
-            row_messages("y2", "recv")
-
-        @pl.when(t == 0)
-        def _():
-            wait_halo(y2, 2, ch, SEM_Y2, False, c, NCH)
-
-        @pl.when(t == 1)
-        def _():
-            wait_halo(y2, 2, ch, SEM_Y2, True, c, NCH)
-
         at = 1 + c * ch
         taps = []
         for first in (at - 1, at, at + 1):
@@ -477,14 +493,31 @@
                 taps.append(flat(y2[k + side, pl.ds(first, ch)]))
         taps.append(flat(z1[2 * k + 3, pl.ds(at, ch), 0]))
         acc = dot(jnp.concatenate(taps, axis=1), w2c[...])
-        val = jnp.maximum(acc + b2c[...], 0.0).astype(BF16).reshape(ch // 2, 2, n, c2)
+        val = relu(acc + b2c[...]).astype(BF16).reshape(ch // 2, 2, n, c2)
         z2[k + 3 - s, pl.ds(1 + c * (ch // 2), ch // 2)] = val
 
-        @pl.when((t == 0) & has_fwd)
+    row_messages("y2", "recv")
+
+    def z2_item(item, carry):
+        c = item - 2 * extra
+
+        @pl.when(c >= 0)
+        def _():
+            wait_halo(y2, 2, ch, SEM_Y2, False, c, NCH)
+            wait_halo(y2, 2, ch, SEM_Y2, True, c, NCH)
+
+        for j in range(2):
+            z2_job(jnp.where(c < 0, -1, j), jnp.where(c < 0, 2 * item + j, c))
+
+        @pl.when((c >= 0) & has_fwd)
         def _():
             z_copy(z2, 2, ch // 2, SEM_Z2, c).start()
-    phase(2, NCH, z2_item)
+        return carry
+    loop(NCH + 2 * extra, z2_item)
     row_messages("z2", "send")
+
+    for copy in w3d_loads:
+        copy.wait()
 
     def y3_item(t, c):
         k = t
@@ -498,16 +531,15 @@
             for j in range(NCH // NCH3):
                 z_recv(z2, 2, ch // 2, SEM_Z2, c * (NCH // NCH3) + j).wait_recv()
 
-        at = 1 + c * ch3
-        acc = jnp.zeros((ch3 * n, c3), F32)
-        tap = 0
-        for first, sub in ((at - 1, 1), (at, 0), (at, 1)):
-            for side in range(3):
-                acc = acc + dot(flat(z2[2 * k + 2 + side, pl.ds(first, ch3), sub]), w3d[tap])
-                tap += 1
-        val = jnp.maximum(acc + b3d[...], 0.0)
-        val = jnp.where(last_void & (t == 0), 0.0, val)
-        y3[k + 2, pl.ds(at, ch3)] = val.astype(BF16).reshape(ch3, n, c3)
+        for at, size in parts(1 + c * ch3, ch3):
+            acc = b3d[...]
+            tap = 0
+            for first, sub in ((at - 1, 1), (at, 0), (at, 1)):
+                for side in range(3):
+                    acc = acc + dot_nt(flat(z2[2 * k + 2 + side, pl.ds(first, size), sub]), w3r[tap])
+                    tap += 1
+            val = jnp.where(last_void & (t == 0), 0.0, relu(acc))
+            y3[k + 2, pl.ds(at, size)] = val.astype(BF16).reshape(size, n, c3)
 
         @pl.when((t == 0) & has_fwd)
         def _():
@@ -549,15 +581,14 @@
             wait_halo(y3, 1, ch3, SEM_Y3, False, c, NCH3)
             wait_halo(y3, 1, ch3, SEM_Y3, True, c, NCH3)
 
-        at = 1 + c * ch3
-        acc = dot(flat(z2[2 * k + 3, pl.ds(at, ch3), 0]), wp3[...])
-        tap = 0
-        for first in (at - 1, at, at + 1):
-            for side in (1, 2, 3):
-                acc = acc + dot(flat(y3[k + side, pl.ds(first, ch3)]), w3c[tap])
-                tap += 1
-        val = jnp.maximum(acc + b3c[...], 0.0)
-        zo[k + 1, pl.ds(c * ch3, ch3)] = val.astype(BF16).reshape(ch3, n, c3)
+        for at, size in parts(1 + c * ch3, ch3):
+            acc = dot_nt(flat(z2[2 * k + 3, pl.ds(at, size), 0]), wp3r[...]) + b3c[...]
+            tap = 0
+            for first in (at - 1, at, at + 1):
+                for side in (1, 2, 3):
+                    acc = acc + dot(flat(y3[k + side, pl.ds(first, size)]), w3c[tap])
+                    tap += 1
+            zo[k + 1, pl.ds(at - 1, size)] = relu(acc).astype(BF16).reshape(size, n, c3)
 
         @pl.when((t == 0) & ships)
         def _():
@@ -643,7 +674,7 @@
                 vm((6, h4 + 1, 4, n, pair), BF16), vm((7, h4 + 2, 2, n, c1), BF16), vm((7, h4 + 1, 2, n, c1), BF16),
                 vm((5, h4 + 2, n, c2), BF16), vm((5, h8 + 1, 2, n, c2), BF16), vm((4, h8 + 2, n, c3), BF16), vm((2, h8, n, c3), BF16),
                 vm((10 * pair, 2 * c1), BF16), vm((12 * c1 + 2 * pair, 2 * c1), BF16), vm((9 * c1, c2), BF16), vm((9 * c2 + c1, c2), BF16),
-                vm((9, c3, c2), BF16), vm((9, c2, c3), BF16), vm((9, c3, c3), BF16), vm((c3, c2), BF16), vm((c2, c3), BF16),
+                vm((9, c3, c2), BF16), vm((9, c3, c3), BF16), vm((c3, c2), BF16),
             ] + [vm((1, width), F32) for width in (c1, c1, c2, c2, c3, c3)] + [
                 dma((count,)) for count in (32, 4, 10 * NCH, 10 * NCH, 12 * MAX_PLAN, 12 * MAX_PLAN, 3 * NCH3)],
             compiler_params=pltpu.CompilerParams(collective_id=0, has_side_effects=True, vmem_limit_bytes=63 * 1024 * 1024),

time: 88.1 us -> 84.9 us (0.964)
  Pallas kernels: 85 us -> 81.8 us
    pallas_call x1, Pallas kernels: 85 us -> 81.8 us  [local_blocks(): pl.pallas_call(functools.partial(kernel, dims), out_shape=jax.ShapeDtypeS...]
where the time goes in v3:
time: 84.9 us; the launch traced here: 83.6 us
  Pallas kernels  81.8 us (96%)
  local copies, waits for them, and re-layouts  1.82 us (2%)
    pallas_call x1, Pallas kernels, local_blocks(): pl.pallas_call(functools.partial(kernel, dims), out_shape=jax.ShapeDtypeS...  81.8 us
    reshape x1, local copies, waits for them, and re-layouts, local_blocks(): return jnp.swapaxes(out, 0, 1).reshape(n, h8, 1, c3)  1.82 us

profile of v3, /device:TPU:13, one launch (start us, length us, event | category | flops | bytes accessed | tf_op | source)
XLA Modules:
  0.0 83.6 jit_solution(17837858176697129974)
XLA Ops:
  0.0 81.8 %shard_map.154 = bf16[32,16,320]{2,1,0:T(8,128)(2,1)} custom-call(bf16[16,4,128,256]{3,2,1,0:T(8,128)(2,1)} %bitcast.16, bf16[3,192,128]{2,1,0:T(8,128)(2,1)} %bitcast.23, bf16[1152,128]{1,0:T(8,128)(2,1)} %bitcast.21, bf16[64,128]{1,0:T(8,128)(2,1)} %wp1_h.1, bf16[1152,256]{1,0:T(8,128)(2,1)} %bitcast.20, bf16[2304,256]{1,0:T(8,128)(2,1)} %bitcast.19, ...), custom_call_target="tpu_custom_call" | custom-call | flops 11274289152 | bytes 16777216 | tf_op jit(solution)/shard_map/pallas_call | solution.py:667
  81.8 1.8 %copy.17 = bf16[16,32,1,320]{3,1,2,0:T(8,128)(2,1)} copy(bf16[16,32,1,320]{3,0,1,2:T(8,128)(2,1)} %bitcast.15) | data formatting | bytes 655360 | tf_op jit(solution)/shard_map/reshape | solution.py:683

commit v4 on v3

--- a/solution.py
+++ b/solution.py
@@ -16,7 +16,9 @@
 MAX_PLAN = 5
 BLOCK = 16
 UNROLL = 4
-OWN, HALO = range(2)
+OWN, HALO = BOTH = range(2)
+AROUND = (1, 2, 3)
+UP, DOWN = (False,), (True,)
 NT = (((1,), (1,)), ((), ()))
 
 
@@ -82,7 +84,7 @@
     x_loads = [load(x_hbm.at[:, q], raw.at[q]) for q in range(PAIRS)]
     w1d_loads = [load(b1d_h, b1d.at[0]), load(b1c_h, b1c.at[0])]
     w1c_loads = []
-    for p in range(2):
+    for p in BOTH:
         lanes = pl.ds(p * c1, c1)
         for kh in range(3):
             w1d_loads.append(load(w1d_h.at[kh], w1d.at[pl.ds((kh + 2 * p) * 2 * pair + c0, 3 * c0), lanes]))
@@ -117,6 +119,12 @@
         return jnp.dot(lhs, rhs, preferred_element_type=F32)
 
     def zero_slot(ref, idx):
+        ref[idx] = jnp.zeros(ref.shape[1:], ref.dtype)
+
+    def dot(lhs, rhs):
+        return jnp.dot(lhs, rhs, preferred_element_type=F32)
+
+    def zero_slot(ref, idx):
         def body(i, carry):
             ref[idx, i] = jnp.zeros(ref.shape[2:], ref.dtype)
             return carry
@@ -129,13 +137,18 @@
 
     @pl.when(col == 0)
     def _():
-        for slots, group in enumerate(((xs, y1, z1, y2, z2, y3), (y1, z1, y2, z2, y3), (z1, z2))):
-            for ref in group:
-                zero_slot(ref, slots)
+        for ref in (y1, y2, y3):
+            zero_slot(ref, 1 - s)
+        for ref in (z1, z2):
+            zero_slot(ref, 2 - 2 * s)
+
+    @pl.when(first_extra)
+    def _():
+        zero_slot(xs, 0)
 
     @pl.when(col == cols - 1)
     def _():
-        for ref in (y1, z1, y2, z2, y3):
+        for ref in (y1, y2, y3):
             zero_slot(ref, ref.shape[0] - 1)
 
     @pl.when(is0 | jnp.logical_not(has_bwd))
@@ -167,7 +180,7 @@
     for shift in SHIFTS:
         @pl.when(has_fwd & (s == shift))
         def _():
-            for half in range(2):
+            for half in BOTH:
                 x_copy(shift, half).start()
 
     def y_copy(ref, width, rows_per, sem0, forward, chunk, nch):
@@ -200,9 +213,9 @@
 
     SEM_Y1, SEM_Z1, SEM_Y2, SEM_Z2, SEM_Y3 = (i * 2 * NCH for i in range(5))
 
-    def row_messages(name, act):
+    def row_messages(name, act, ways=None):
         kind, width, sem0 = ROW_SEM[name]
-        for down in directions(name):
+        for down in ways or directions(name):
             for s_send, s_recv in zip(SHIFTS, reversed(SHIFTS)):
                 step = 1 if down else -1
                 for i, (dist, src, dst, count, extra) in enumerate(row_plan(kind, width, s_send, s_recv)):
@@ -232,6 +245,15 @@
                             else:
                                 copy.wait_send()
 
+    def send_edges(name, chunk, nch):
+        @pl.when(chunk == 0)
+        def _():
+            row_messages(name, "send", UP)
+
+        @pl.when(chunk == nch - 1)
+        def _():
+            row_messages(name, "send", DOWN)
+
     def unit_where(size, source):
         at = lax.broadcasted_iota(jnp.int32, (size, size), 0)
         return (at == source(lax.broadcasted_iota(jnp.int32, (size, size), 1))).astype(F32).astype(BF16)
@@ -256,7 +278,7 @@
                 at = i * UNROLL + j
                 block = turned[:, pl.ds(at * BLOCK, BLOCK), :].reshape(n * BLOCK, 2 * pair)
                 moved = dot(mix[...], block)
-                for side in range(2):
+                for side in BOTH:
                     xs[q + 2 - s + side, pl.ds(1 + at * (BLOCK // 4), BLOCK // 4)] = to_rows(moved[:, side * pair:(side + 1) * pair])
             return carry
         loop(h // BLOCK // UNROLL, place)
@@ -270,15 +292,15 @@
                 at = 2 * (i * UNROLL + j)
                 block = xh[half, pl.ds(at, 2)].reshape(2 * pair, hh)
                 both = lax.dot_general(unit, block, NT, preferred_element_type=F32).astype(BF16)
-                for side in range(2):
+                for side in BOTH:
                     turned[at + side, :hh, :pair] = both[:, side * pair:(side + 1) * pair]
             return carry
         loop(n // 2 // UNROLL, turn)
 
         def place(i, carry):
-            blocks = [turned[:, pl.ds((2 * i + j) * BLOCK, BLOCK), :pair].reshape(n * BLOCK, pair) for j in range(2)]
+            blocks = [turned[:, pl.ds((2 * i + j) * BLOCK, BLOCK), :pair].reshape(n * BLOCK, pair) for j in BOTH]
             moved = dot(mix[...], jnp.concatenate(blocks, axis=1))
-            for j in range(2):
+            for j in BOTH:
                 first = 1 + half * (h4 // 2) + (2 * i + j) * (BLOCK // 4)
                 xs[slot, pl.ds(first, BLOCK // 4)] = to_rows(moved[:, j * pair:(j + 1) * pair])
             return carry
@@ -288,7 +310,7 @@
         ref[pl.ds(first, size), pl.ds(p * c1, c1)] = jnp.zeros((size, c1), BF16)
 
     def zero_weights():
-        for p in range(2):
+        for p in BOTH:
             for kh in range(5):
                 tap_at = kh * 2 * pair
                 used = 2 * p <= kh < 2 * p + 3
@@ -307,10 +329,13 @@
 
     def parts(first, count):
         size = count // 2
-        return tuple((first + i * size, size) for i in range(2))
+        return tuple((first + i * size, size) for i in BOTH)
 
     def dot_nt(lhs, rhs):
         return lax.dot_general(lhs, rhs, NT, preferred_element_type=F32)
+
+    def rows_down(at):
+        return (at - 1, 1), (at, 0), (at, 1)
 
     def own_col(t, width):
         return jnp.where(is0, width - 1 - t, t)
@@ -331,7 +356,7 @@
                 taps.append(flat(xs[k + side, pl.ds(first, ch), sub]))
         acc = dot(jnp.concatenate(taps, axis=1), w1d[...])
         void = last_void & (t == 3)
-        for p in range(2):
+        for p in BOTH:
             val = relu(acc[:, p * c1:(p + 1) * c1] + b1d[...])
             val = jnp.where(void, 0.0, val)
             y1[k + 2, pl.ds(at, ch), p] = val.astype(BF16).reshape(ch, n, c1)
@@ -360,13 +385,15 @@
             turn_halo(half)
 
         jobs = []
-        for j in range(2):
+        for j in BOTH:
             at = 2 * item + j
             t = jnp.where(at < 3 * early, lax.div(at, 3) + t_first, jnp.where(half >= 0, 3, at - 3 * early + t_first))
             c = jnp.where(at < 3 * early, lax.rem(at, 3) + 1, jnp.where(half >= 0, at - NCH * early, 0))
             jobs.append((t, c))
         for t, c in jobs:
             y1_job(t, c)
+        send_edges("y1", half, 2)
+
         for t, c in jobs:
             @pl.when((t == 0) & has_fwd)
             def _():
@@ -377,7 +404,6 @@
                 y_copy(y1, PAIRS, ch, SEM_Y1, False, c, NCH).start()
         return carry
     loop(2 * (PAIRS - t_first), y1_item)
-    row_messages("y1", "send")
     for copy in w1c_loads:
         copy.wait()
 
@@ -397,12 +423,12 @@
         at = 1 + c * ch
         taps = []
         for first, sub in ((at - 1, 1), (at, 0), (at, 1), (at + 1, 0)):
-            for side in (1, 2, 3):
+            for side in AROUND:
                 taps.append(flat(y1[k + side, pl.ds(first, ch), sub]))
         for sub in (0, 2):
             taps.append(flat(xs[k + 2, pl.ds(at, ch), sub]))
         acc = dot(jnp.concatenate(taps, axis=1), w1c[...])
-        for p in range(2):
+        for p in BOTH:
             val = relu(acc[:, p * c1:(p + 1) * c1] + b1c[...])
             z1[k + 3 - s, pl.ds(at, ch), p] = val.astype(BF16).reshape(ch, n, c1)
 
@@ -423,7 +449,7 @@
             wait_halo(y1, PAIRS, ch, SEM_Y1, True, edge, NCH)
 
         mid = jnp.where(inner < 2, inner + 1, jnp.where(inner == 2, 0, inner))
-        for j in range(2):
+        for j in BOTH:
             t = jnp.where(more, -1, jnp.where(edge >= 0, 3 * j, j + 1))
             c = jnp.where(more, jnp.where(inner < 0, j + 1, 3 * j), jnp.where(edge >= 0, edge, mid))
             z1_job(t, c)
@@ -440,7 +466,7 @@
     def y2_job(t, at, size):
         k = own_col(t, 2)
         taps = []
-        for first, sub in ((at - 1, 1), (at, 0), (at, 1)):
+        for first, sub in rows_down(at):
             for side in range(3):
                 taps.append(flat(z1[2 * k + 2 + side, pl.ds(first, size), sub]))
         acc = dot(jnp.concatenate(taps, axis=1), w2d[...])
@@ -475,12 +501,13 @@
         for at, size in parts(1 + c * ch, ch):
             y2_job(jnp.int32(1), at, size)
 
+        send_edges("y2", c, NCH)
+
         @pl.when(has_bwd)
         def _():
             y_copy(y2, 2, ch, SEM_Y2, False, c, NCH).start()
         return carry
     loop(NCH, y2_edge)
-    row_messages("y2", "send")
     for copy in w2c_loads:
         copy.wait()
 
@@ -489,7 +516,7 @@
         at = 1 + c * ch
         taps = []
         for first in (at - 1, at, at + 1):
-            for side in (1, 2, 3):
+            for side in AROUND:
                 taps.append(flat(y2[k + side, pl.ds(first, ch)]))
         taps.append(flat(z1[2 * k + 3, pl.ds(at, ch), 0]))
         acc = dot(jnp.concatenate(taps, axis=1), w2c[...])
@@ -506,7 +533,7 @@
             wait_halo(y2, 2, ch, SEM_Y2, False, c, NCH)
             wait_halo(y2, 2, ch, SEM_Y2, True, c, NCH)
 
-        for j in range(2):
+        for j in BOTH:
             z2_job(jnp.where(c < 0, -1, j), jnp.where(c < 0, 2 * item + j, c))
 
         @pl.when((c >= 0) & has_fwd)
@@ -534,13 +561,17 @@
         for at, size in parts(1 + c * ch3, ch3):
             acc = b3d[...]
             tap = 0
-            for first, sub in ((at - 1, 1), (at, 0), (at, 1)):
+            for first, sub in rows_down(at):
                 for side in range(3):
                     acc = acc + dot_nt(flat(z2[2 * k + 2 + side, pl.ds(first, size), sub]), w3r[tap])
                     tap += 1
             val = jnp.where(last_void & (t == 0), 0.0, relu(acc))
             y3[k + 2, pl.ds(at, size)] = val.astype(BF16).reshape(size, n, c3)
 
+        @pl.when(t == 0)
+        def _():
+            send_edges("y3", c, NCH3)
+
         @pl.when((t == 0) & has_fwd)
         def _():
             y_copy(y3, 1, ch3, SEM_Y3, True, c, NCH3).start()
@@ -549,7 +580,6 @@
         def _():
             y_copy(y3, 1, ch3, SEM_Y3, False, c, NCH3).start()
     phase(1, NCH3, y3_item)
-    row_messages("y3", "send")
     for copy in w3c_loads:
         copy.wait()
 
@@ -585,7 +615,7 @@
             acc = dot_nt(flat(z2[2 * k + 3, pl.ds(at, size), 0]), wp3r[...]) + b3c[...]
             tap = 0
             for first in (at - 1, at, at + 1):
-                for side in (1, 2, 3):
+                for side in AROUND:
                     acc = acc + dot(flat(y3[k + side, pl.ds(first, size)]), w3c[tap])
                     tap += 1
             zo[k + 1, pl.ds(at - 1, size)] = relu(acc).astype(BF16).reshape(size, n, c3)
@@ -602,7 +632,7 @@
     for shift in SHIFTS:
         @pl.when(has_fwd & (s == shift))
         def _():
-            for half in range(2):
+            for half in BOTH:
                 x_copy(shift, half).wait_send()
 
     def drain(c, carry):
@@ -670,11 +700,12 @@
             in_specs=[pl.BlockSpec(memory_space=pl.ANY)] * len(args),
             out_specs=pl.BlockSpec(memory_space=pl.ANY),
             scratch_shapes=[
-                vm((PAIRS, n, pair, h), BF16), vm((2, n, pair, h // 2), BF16), vm((n, h, 2 * pair), BF16), vm((h, h), BF16), vm((n * BLOCK, n * BLOCK), BF16),
-                vm((6, h4 + 1, 4, n, pair), BF16), vm((7, h4 + 2, 2, n, c1), BF16), vm((7, h4 + 1, 2, n, c1), BF16),
-                vm((5, h4 + 2, n, c2), BF16), vm((5, h8 + 1, 2, n, c2), BF16), vm((4, h8 + 2, n, c3), BF16), vm((2, h8, n, c3), BF16),
-                vm((10 * pair, 2 * c1), BF16), vm((12 * c1 + 2 * pair, 2 * c1), BF16), vm((9 * c1, c2), BF16), vm((9 * c2 + c1, c2), BF16),
-                vm((9, c3, c2), BF16), vm((9, c3, c3), BF16), vm((c3, c2), BF16),
+                vm(shape, BF16) for shape in (
+                    (PAIRS, n, pair, h), (2, n, pair, h // 2), (n, h, 2 * pair), (h, h), (n * BLOCK, n * BLOCK),
+                    (6, h4 + 1, 4, n, pair), (7, h4 + 2, 2, n, c1), (7, h4 + 1, 2, n, c1),
+                    (5, h4 + 2, n, c2), (5, h8 + 1, 2, n, c2), (4, h8 + 2, n, c3), (2, h8, n, c3),
+                    (10 * pair, 2 * c1), (12 * c1 + 2 * pair, 2 * c1), (9 * c1, c2), (9 * c2 + c1, c2),
+                    (9, c3, c2), (9, c3, c3), (c3, c2))
             ] + [vm((1, width), F32) for width in (c1, c1, c2, c2, c3, c3)] + [
                 dma((count,)) for count in (32, 4, 10 * NCH, 10 * NCH, 12 * MAX_PLAN, 12 * MAX_PLAN, 3 * NCH3)],
             compiler_params=pltpu.CompilerParams(collective_id=0, has_side_effects=True, vmem_limit_bytes=63 * 1024 * 1024),

time: 84.9 us -> 77.3 us (0.910); the launches traced: 83.6 us -> 77.2 us
  Pallas kernels: 81.8 us -> 75.4 us
    pallas_call x1, Pallas kernels: 81.8 us -> 75.4 us  [local_blocks(): pl.pallas_call(functools.partial(kernel, dims), out_shape=jax.ShapeDtypeS...]
where the time goes in v4:
time: 77.3 us; the launch traced here: 77.2 us
  Pallas kernels  75.4 us (98%)
  local copies, waits for them, and re-layouts  1.82 us (2%)
    pallas_call x1, Pallas kernels, local_blocks(): pl.pallas_call(functools.partial(kernel, dims), out_shape=jax.ShapeDtypeS...  75.4 us
    reshape x1, local copies, waits for them, and re-layouts, local_blocks(): return jnp.swapaxes(out, 0, 1).reshape(n, h8, 1, c3)  1.82 us

profile of v4, /device:TPU:13, one launch (start us, length us, event | category | flops | bytes accessed | tf_op | source)
XLA Modules:
  0.0 77.2 jit_solution(13704989086910704453)
XLA Ops:
  0.0 75.4 %shard_map.154 = bf16[32,16,320]{2,1,0:T(8,128)(2,1)} custom-call(bf16[16,4,128,256]{3,2,1,0:T(8,128)(2,1)} %bitcast.16, bf16[3,192,128]{2,1,0:T(8,128)(2,1)} %bitcast.23, bf16[1152,128]{1,0:T(8,128)(2,1)} %bitcast.21, bf16[64,128]{1,0:T(8,128)(2,1)} %wp1_h.1, bf16[1152,256]{1,0:T(8,128)(2,1)} %bitcast.20, bf16[2304,256]{1,0:T(8,128)(2,1)} %bitcast.19, ...), custom_call_target="tpu_custom_call" | custom-call | flops 11274289152 | bytes 16777216 | tf_op jit(solution)/shard_map/pallas_call | solution.py:697
  75.4 1.8 %copy.17 = bf16[16,32,1,320]{3,1,2,0:T(8,128)(2,1)} copy(bf16[16,32,1,320]{3,0,1,2:T(8,128)(2,1)} %bitcast.15) | data formatting | bytes 655360 | tf_op jit(solution)/shard_map/reshape | solution.py:714

commit v5 on v4

--- a/solution.py
+++ b/solution.py
@@ -94,7 +94,7 @@
     w2c_loads = [load(w2c_h, w2c.at[pl.ds(0, k2)]), load(wp2_h, w2c.at[pl.ds(k2, c1)]), load(b2c_h, b2c.at[0])]
     w3d_loads = [load(w3d_h, w3r), load(b3d_h, b3d.at[0]), load(wp3_h, wp3r)]
     w3c_loads = [load(w3c_h, w3c), load(b3c_h, b3c.at[0])]
-    for copy in x_loads + w1d_loads + w1c_loads + w2d_loads + w2c_loads + w3d_loads + w3c_loads:
+    for copy in x_loads:
         copy.start()
 
     def row_refs(name, slots, down, side):
@@ -160,10 +160,37 @@
         loop(n, body)
 
     barrier = pltpu.get_barrier_semaphore()
-    for rr in range(rows):
-        for cc in range(cols):
-            pl.semaphore_signal(barrier, inc=1, device_id={"row": jnp.int32(rr), "col": jnp.int32(cc)}, device_id_type=pl.DeviceIdType.MESH)
-    pl.semaphore_wait(barrier, rows * cols)
+    around = 0
+    for step in range(-1, 2):
+        for dist in range(-2, 3):
+            near_row, near_col = row + step, col + dist
+            ok = (near_row >= 0) & (near_row < rows) & (near_col >= 0) & (near_col < cols)
+            around = around + ok.astype(jnp.int32)
+
+            @pl.when(ok)
+            def _():
+                pl.semaphore_signal(barrier, inc=1, device_id={"row": near_row, "col": near_col}, device_id_type=pl.DeviceIdType.MESH)
+
+    def unit_where(size, source):
+        at = lax.broadcasted_iota(jnp.int32, (size, size), 0)
+        return (at == source(lax.broadcasted_iota(jnp.int32, (size, size), 1))).astype(F32).astype(BF16)
+
+    eye[...] = unit_where(h, lambda at: at)
+    mix[...] = unit_where(n * BLOCK, lambda at: (at & (BLOCK - 1)) * n + (at >> BLOCK.bit_length() - 1))
+
+    def zero_part(ref, first, size, p):
+        ref[pl.ds(first, size), pl.ds(p * c1, c1)] = jnp.zeros((size, c1), BF16)
+
+    for p in BOTH:
+        for kh in range(5):
+            tap_at = kh * 2 * pair
+            used = 2 * p <= kh < 2 * p + 3
+            zero_part(w1d, tap_at, c0 if used else 2 * pair, p)
+        zero_part(w1c, (1 - p) * k1, 3 * c1, p)
+        proj_at = 12 * c1
+        zero_part(w1c, proj_at + (1 - p) * pair, pair, p)
+        zero_part(w1c, proj_at + p * pair + c0, c0, p)
+    pl.semaphore_wait(barrier, around)
 
     def remote(src, dst, send_sem, recv_sem, to_row, to_col):
         return pltpu.make_async_remote_copy(src_ref=src, dst_ref=dst, send_sem=send_sem, recv_sem=recv_sem,
@@ -254,13 +281,6 @@
         def _():
             row_messages(name, "send", DOWN)
 
-    def unit_where(size, source):
-        at = lax.broadcasted_iota(jnp.int32, (size, size), 0)
-        return (at == source(lax.broadcasted_iota(jnp.int32, (size, size), 1))).astype(F32).astype(BF16)
-
-    eye[...] = unit_where(h, lambda at: at)
-    mix[...] = unit_where(n * BLOCK, lambda at: (at & (BLOCK - 1)) * n + (at >> BLOCK.bit_length() - 1))
-
     def to_rows(value):
         return value.astype(BF16).reshape(BLOCK // 4, 4, n, pair)
 
@@ -306,22 +326,9 @@
             return carry
         loop(hh // BLOCK // 2, place)
 
-    def zero_part(ref, first, size, p):
-        ref[pl.ds(first, size), pl.ds(p * c1, c1)] = jnp.zeros((size, c1), BF16)
-
-    def zero_weights():
-        for p in BOTH:
-            for kh in range(5):
-                tap_at = kh * 2 * pair
-                used = 2 * p <= kh < 2 * p + 3
-                zero_part(w1d, tap_at, c0 if used else 2 * pair, p)
-            zero_part(w1c, (1 - p) * k1, 3 * c1, p)
-            proj_at = 12 * c1
-            zero_part(w1c, proj_at + (1 - p) * pair, pair, p)
-            zero_part(w1c, proj_at + p * pair + c0, c0, p)
-
-    zero_weights()
-    for copy in x_loads + w1d_loads:
+    for copy in w1d_loads + w1c_loads + w2d_loads + w2c_loads + w3d_loads + w3c_loads:
+        copy.start()
+    for copy in x_loads:
         copy.wait()
 
     def flat(value):
@@ -366,6 +373,8 @@
         return carry
     loop(PAIRS // 2, own_group)
     row_messages("x", "send")
+    for copy in w1d_loads:
+        copy.wait()
     early = 3 - t_first
 
     def y1_item(item, carry):
@@ -407,16 +416,18 @@
     for copy in w1c_loads:
         copy.wait()
 
-    def wait_halo(ref, width, rows_per, sem0, forward, c, nch):
+    def wait_halo(ref, width, rows_per, sem0, forward, half, nch):
         exists = has_bwd if forward else has_fwd
 
-        @pl.when(exists & (c == 0))
-        def _():
-            y_recv(ref, width, rows_per, sem0, forward, 0, nch).wait_recv()
-
-        @pl.when(exists & (c < nch - 1))
-        def _():
-            y_recv(ref, width, rows_per, sem0, forward, c + 1, nch).wait_recv()
+        @pl.when(exists & (half == 0))
+        def _():
+            for c in range(nch - nch // 4):
+                y_recv(ref, width, rows_per, sem0, forward, c, nch).wait_recv()
+
+        @pl.when(exists & (half == 1))
+        def _():
+            for c in range(nch - nch // 4, nch):
+                y_recv(ref, width, rows_per, sem0, forward, c, nch).wait_recv()
 
     def z1_job(t, c):
         k = own_col(t, PAIRS)
@@ -443,20 +454,28 @@
         def _():
             row_messages("y1", "recv")
 
-        @pl.when(edge >= 0)
-        def _():
-            wait_halo(y1, PAIRS, ch, SEM_Y1, False, edge, NCH)
-            wait_halo(y1, PAIRS, ch, SEM_Y1, True, edge, NCH)
+        half = lax.rem(edge, 2)
+        far = edge >= 2
+
+        @pl.when((edge >= 0) & (edge < 2))
+        def _():
+            wait_halo(y1, PAIRS, ch, SEM_Y1, False, half, NCH)
+
+        @pl.when(far)
+        def _():
+            wait_halo(y1, PAIRS, ch, SEM_Y1, True, half, NCH)
 
         mid = jnp.where(inner < 2, inner + 1, jnp.where(inner == 2, 0, inner))
+        edge_col = jnp.where(far, 3, 0)
         for j in BOTH:
-            t = jnp.where(more, -1, jnp.where(edge >= 0, 3 * j, j + 1))
-            c = jnp.where(more, jnp.where(inner < 0, j + 1, 3 * j), jnp.where(edge >= 0, edge, mid))
+            t = jnp.where(more, -1, jnp.where(edge >= 0, edge_col, j + 1))
+            c = jnp.where(more, jnp.where(inner < 0, j + 1, 3 * j), jnp.where(edge >= 0, 2 * half + j, mid))
             z1_job(t, c)
 
-        @pl.when((edge >= 0) & has_fwd)
-        def _():
-            z_copy(z1, PAIRS, ch, SEM_Z1, edge).start()
+        @pl.when((edge >= 0) & (edge < 2) & has_fwd)
+        def _():
+            for j in BOTH:
+                z_copy(z1, PAIRS, ch, SEM_Z1, 2 * half + j).start()
         return carry
     loop(2 * (NCH + extra), z1_item)
     row_messages("z1", "send")
@@ -526,19 +545,25 @@
     row_messages("y2", "recv")
 
     def z2_item(item, carry):
-        c = item - 2 * extra
-
-        @pl.when(c >= 0)
-        def _():
-            wait_halo(y2, 2, ch, SEM_Y2, False, c, NCH)
-            wait_halo(y2, 2, ch, SEM_Y2, True, c, NCH)
+        edge = item - 2 * extra
+        half = lax.rem(item, 2)
+        near = (edge >= 0) & (edge < 2)
+
+        @pl.when(near)
+        def _():
+            wait_halo(y2, 2, ch, SEM_Y2, False, half, NCH)
+
+        @pl.when(edge >= 2)
+        def _():
+            wait_halo(y2, 2, ch, SEM_Y2, True, half, NCH)
 
         for j in BOTH:
-            z2_job(jnp.where(c < 0, -1, j), jnp.where(c < 0, 2 * item + j, c))
-
-        @pl.when((c >= 0) & has_fwd)
-        def _():
-            z_copy(z2, 2, ch // 2, SEM_Z2, c).start()
+            z2_job(lax.div(edge + 2, 2) - 1, 2 * half + j)
+
+        @pl.when(near & has_fwd)
+        def _():
+            for j in BOTH:
+                z_copy(z2, 2, ch // 2, SEM_Z2, 2 * half + j).start()
         return carry
     loop(NCH + 2 * extra, z2_item)
     row_messages("z2", "send")
@@ -606,10 +631,13 @@
         def _():
             row_messages("y3", "recv")
 
-        @pl.when(t == 0)
-        def _():
-            wait_halo(y3, 1, ch3, SEM_Y3, False, c, NCH3)
-            wait_halo(y3, 1, ch3, SEM_Y3, True, c, NCH3)
+        @pl.when((t == 0) & (c == 0))
+        def _():
+            for forward, exists in ((False, has_fwd), (True, has_bwd)):
+                @pl.when(exists)
+                def _():
+                    for chunk in range(NCH3):
+                        y_recv(y3, 1, ch3, SEM_Y3, forward, chunk, NCH3).wait_recv()
 
         for at, size in parts(1 + c * ch3, ch3):
             acc = dot_nt(flat(z2[2 * k + 3, pl.ds(at, size), 0]), wp3r[...]) + b3c[...]

time: 77.3 us -> 74.9 us (0.969)
  Pallas kernels: 75.4 us -> 72.9 us
    pallas_call x1, Pallas kernels: 75.4 us -> 72.9 us  [local_blocks(): pl.pallas_call(functools.partial(kernel, dims), out_shape=jax.ShapeDtypeS...]
where the time goes in v5:
time: 74.9 us; the launch traced here: 74.7 us
  Pallas kernels  72.9 us (97%)
  local copies, waits for them, and re-layouts  1.82 us (2%)
    pallas_call x1, Pallas kernels, local_blocks(): pl.pallas_call(functools.partial(kernel, dims), out_shape=jax.ShapeDtypeS...  72.9 us
    reshape x1, local copies, waits for them, and re-layouts, local_blocks(): return jnp.swapaxes(out, 0, 1).reshape(n, h8, 1, c3)  1.82 us

profile of v5, /device:TPU:13, one launch (start us, length us, event | category | flops | bytes accessed | tf_op | source)
XLA Modules:
  0.0 74.7 jit_solution(6539500750203103796)
XLA Ops:
  0.0 72.9 %shard_map.154 = bf16[32,16,320]{2,1,0:T(8,128)(2,1)} custom-call(bf16[16,4,128,256]{3,2,1,0:T(8,128)(2,1)} %bitcast.16, bf16[3,192,128]{2,1,0:T(8,128)(2,1)} %bitcast.23, bf16[1152,128]{1,0:T(8,128)(2,1)} %bitcast.21, bf16[64,128]{1,0:T(8,128)(2,1)} %wp1_h.1, bf16[1152,256]{1,0:T(8,128)(2,1)} %bitcast.20, bf16[2304,256]{1,0:T(8,128)(2,1)} %bitcast.19, ...), custom_call_target="tpu_custom_call" | custom-call | flops 11274289152 | bytes 16777216 | tf_op jit(solution)/shard_map/pallas_call | solution.py:725
  72.9 1.8 %copy.17 = bf16[16,32,1,320]{3,1,2,0:T(8,128)(2,1)} copy(bf16[16,32,1,320]{3,0,1,2:T(8,128)(2,1)} %bitcast.15) | data formatting | bytes 655360 | tf_op jit(solution)/shard_map/reshape | solution.py:742

commit v6 on v5

--- a/solution.py
+++ b/solution.py
@@ -18,6 +18,7 @@
 UNROLL = 4
 OWN, HALO = BOTH = range(2)
 AROUND = (1, 2, 3)
+NEAR = range(-2, 3)
 UP, DOWN = (False,), (True,)
 NT = (((1,), (1,)), ((), ()))
 
@@ -44,7 +45,7 @@
         need = (-1, width - 1) if s_recv == 0 else (0, width + 1)
         src_at, dst_at = 3 - 2 * s_send, 3 - 2 * s_recv
     plan = []
-    for dist in range(-2, 3):
+    for dist in NEAR:
         lo = max(own[0], width * dist + need[0])
         hi = min(own[1], width * dist + need[1])
         if lo <= hi:
@@ -55,7 +56,7 @@
 
 
 def kernel(dims, x_hbm, w1d_h, w1c_h, wp1_h, w2d_h, w2c_h, wp2_h, w3d_h, w3c_h, wp3_h, b1d_h, b1c_h, b2d_h, b2c_h, b3d_h, b3c_h, out_hbm,
-           raw, xh, turned, eye, mix, xs, y1, z1, y2, z2, y3, zo, w1d, w1c, w2d, w2c, w3r, w3c, wp3r,
+           raw, xh, turned, eye, mix, xs, y1, z1, y2, z2, y3, zo, w1d, w1c, w2d, w2c, w3r, w3d, w3c, w3e, wp3r,
            b1d, b1c, b2d, b2c, b3d, b3c, load_sem, x_sem, col_send, col_recv, row_send, row_recv, out_sem):
     n, h, c0, c1, c2, c3, rows, cols = dims
     h4, h8 = h // 4, h // 8
@@ -93,7 +94,7 @@
     w2d_loads = [load(w2d_h, w2d), load(b2d_h, b2d.at[0])]
     w2c_loads = [load(w2c_h, w2c.at[pl.ds(0, k2)]), load(wp2_h, w2c.at[pl.ds(k2, c1)]), load(b2c_h, b2c.at[0])]
     w3d_loads = [load(w3d_h, w3r), load(b3d_h, b3d.at[0]), load(wp3_h, wp3r)]
-    w3c_loads = [load(w3c_h, w3c), load(b3c_h, b3c.at[0])]
+    w3c_loads = [load(w3c_h.at[:, pl.ds(0, c2)], w3c), load(w3c_h.at[:, pl.ds(c2, c3 - c2)], w3e), load(b3c_h, b3c.at[0])]
     for copy in x_loads:
         copy.start()
 
@@ -135,6 +136,23 @@
             edge = row_refs(name, slice(None), down, HALO)
             edge[...] = jnp.zeros(edge.shape, BF16)
 
+    @pl.when(col == cols - 1)
+    def _():
+        for ref in (y1, y2, y3):
+            zero_slot(ref, ref.shape[0] - 1)
+
+    barrier = pltpu.get_barrier_semaphore()
+    around = 0
+    for step in range(-1, 2):
+        for dist in NEAR:
+            near_row, near_col = row + step, col + dist
+            ok = (near_row >= 0) & (near_row < rows) & (near_col >= 0) & (near_col < cols)
+            around = around + ok.astype(jnp.int32)
+
+            @pl.when(ok)
+            def _():
+                pl.semaphore_signal(barrier, inc=1, device_id={"row": near_row, "col": near_col}, device_id_type=pl.DeviceIdType.MESH)
+
     @pl.when(col == 0)
     def _():
         for ref in (y1, y2, y3):
@@ -146,30 +164,20 @@
     def _():
         zero_slot(xs, 0)
 
-    @pl.when(col == cols - 1)
-    def _():
-        for ref in (y1, y2, y3):
-            zero_slot(ref, ref.shape[0] - 1)
-
-    @pl.when(is0 | jnp.logical_not(has_bwd))
-    def _():
+    def zero_xh(first, size):
         def body(i, carry):
-            xh[0, i] = jnp.zeros((2 * c0, hh), BF16)
-            xh[1, i] = jnp.zeros((2 * c0, hh), BF16)
+            for half in BOTH:
+                xh[half, i, pl.ds(first, size)] = jnp.zeros((size, hh), BF16)
             return carry
         loop(n, body)
 
-    barrier = pltpu.get_barrier_semaphore()
-    around = 0
-    for step in range(-1, 2):
-        for dist in range(-2, 3):
-            near_row, near_col = row + step, col + dist
-            ok = (near_row >= 0) & (near_row < rows) & (near_col >= 0) & (near_col < cols)
-            around = around + ok.astype(jnp.int32)
-
-            @pl.when(ok)
-            def _():
-                pl.semaphore_signal(barrier, inc=1, device_id={"row": near_row, "col": near_col}, device_id_type=pl.DeviceIdType.MESH)
+    @pl.when(is0)
+    def _():
+        zero_xh(0, c0)
+
+    @pl.when(jnp.logical_not(has_bwd))
+    def _():
+        zero_xh(0, pair)
 
     def unit_where(size, source):
         at = lax.broadcasted_iota(jnp.int32, (size, size), 0)
@@ -343,6 +351,9 @@
 
     def rows_down(at):
         return (at - 1, 1), (at, 0), (at, 1)
+
+    def whole(c):
+        return ((1 + c * ch3, ch3),)
 
     def own_col(t, width):
         return jnp.where(is0, width - 1 - t, t)
@@ -419,15 +430,12 @@
     def wait_halo(ref, width, rows_per, sem0, forward, half, nch):
         exists = has_bwd if forward else has_fwd
 
-        @pl.when(exists & (half == 0))
-        def _():
-            for c in range(nch - nch // 4):
-                y_recv(ref, width, rows_per, sem0, forward, c, nch).wait_recv()
-
-        @pl.when(exists & (half == 1))
-        def _():
-            for c in range(nch - nch // 4, nch):
-                y_recv(ref, width, rows_per, sem0, forward, c, nch).wait_recv()
+        split = nch - nch // 4
+        for part in BOTH:
+            @pl.when(exists & (half == part))
+            def _():
+                for c in range(split, nch) if part else range(split):
+                    y_recv(ref, width, rows_per, sem0, forward, c, nch).wait_recv()
 
     def z1_job(t, c):
         k = own_col(t, PAIRS)
@@ -445,6 +453,12 @@
 
     extra = -t_first
 
+    def turn_weight(i, carry):
+        for j in range(3):
+            tap = 3 * i + j
+            w3d[tap] = dot_nt(eye[:c2, :c2], w3r[tap]).astype(BF16)
+        return carry
+
     def z1_item(item, carry):
         inner = item - extra
         edge = inner - NCH - extra
@@ -456,6 +470,12 @@
 
         half = lax.rem(edge, 2)
         far = edge >= 2
+
+        @pl.when(edge == 0)
+        def _():
+            for copy in w3d_loads:
+                copy.wait()
+            loop(3, turn_weight)
 
         @pl.when((edge >= 0) & (edge < 2))
         def _():
@@ -568,9 +588,6 @@
     loop(NCH + 2 * extra, z2_item)
     row_messages("z2", "send")
 
-    for copy in w3d_loads:
-        copy.wait()
-
     def y3_item(t, c):
         k = t
 
@@ -583,13 +600,9 @@
             for j in range(NCH // NCH3):
                 z_recv(z2, 2, ch // 2, SEM_Z2, c * (NCH // NCH3) + j).wait_recv()
 
-        for at, size in parts(1 + c * ch3, ch3):
-            acc = b3d[...]
-            tap = 0
-            for first, sub in rows_down(at):
-                for side in range(3):
-                    acc = acc + dot_nt(flat(z2[2 * k + 2 + side, pl.ds(first, size), sub]), w3r[tap])
-                    tap += 1
+        for at, size in whole(c):
+            taps = [flat(z2[2 * k + 2 + side, pl.ds(first, size), sub]) for first, sub in rows_down(at) for side in range(3)]
+            acc = dot(jnp.concatenate(taps, axis=1), w3d[...].reshape(k2, c3)) + b3d[...]
             val = jnp.where(last_void & (t == 0), 0.0, relu(acc))
             y3[k + 2, pl.ds(at, size)] = val.astype(BF16).reshape(size, n, c3)
 
@@ -639,13 +652,11 @@
                     for chunk in range(NCH3):
                         y_recv(y3, 1, ch3, SEM_Y3, forward, chunk, NCH3).wait_recv()
 
-        for at, size in parts(1 + c * ch3, ch3):
+        for at, size in whole(c):
             acc = dot_nt(flat(z2[2 * k + 3, pl.ds(at, size), 0]), wp3r[...]) + b3c[...]
-            tap = 0
-            for first in (at - 1, at, at + 1):
-                for side in AROUND:
-                    acc = acc + dot(flat(y3[k + side, pl.ds(first, size)]), w3c[tap])
-                    tap += 1
+            taps = [flat(y3[k + side, pl.ds(first, size)]) for first in (at - 1, at, at + 1) for side in AROUND]
+            acc = acc + dot(jnp.concatenate([tap[:, :c2] for tap in taps], axis=1), w3c[...].reshape(k2, c3))
+            acc = acc + dot(jnp.concatenate([tap[:, c2:] for tap in taps], axis=1), w3e[...].reshape(9 * (c3 - c2), c3))
             zo[k + 1, pl.ds(at - 1, size)] = relu(acc).astype(BF16).reshape(size, n, c3)
 
         @pl.when((t == 0) & ships)
@@ -721,7 +732,7 @@
                 b1d, b1c, b2d, b2c, b3d, b3c)
         vm = pltpu.VMEM
         dma = pltpu.SemaphoreType.DMA
-        flops = 2 * n * h * w * c1 * 7 * (c0 + c1)
+        flops = 14 * x.size * (c0 + c1)
         out = pl.pallas_call(
             functools.partial(kernel, dims),
             out_shape=jax.ShapeDtypeStruct((h8, n, c3), BF16),
@@ -733,11 +744,11 @@
                     (6, h4 + 1, 4, n, pair), (7, h4 + 2, 2, n, c1), (7, h4 + 1, 2, n, c1),
                     (5, h4 + 2, n, c2), (5, h8 + 1, 2, n, c2), (4, h8 + 2, n, c3), (2, h8, n, c3),
                     (10 * pair, 2 * c1), (12 * c1 + 2 * pair, 2 * c1), (9 * c1, c2), (9 * c2 + c1, c2),
-                    (9, c3, c2), (9, c3, c3), (c3, c2))
+                    (9, c3, c2), (9, c2, c3), (9, c2, c3), (9, c3 - c2, c3), (c3, c2))
             ] + [vm((1, width), F32) for width in (c1, c1, c2, c2, c3, c3)] + [
                 dma((count,)) for count in (32, 4, 10 * NCH, 10 * NCH, 12 * MAX_PLAN, 12 * MAX_PLAN, 3 * NCH3)],
-            compiler_params=pltpu.CompilerParams(collective_id=0, has_side_effects=True, vmem_limit_bytes=63 * 1024 * 1024),
-            cost_estimate=pl.CostEstimate(flops=flops, bytes_accessed=16 * 1024 * 1024, transcendentals=0),
+            compiler_params=pltpu.CompilerParams(collective_id=0, has_side_effects=True, vmem_limit_bytes=63 << 20),
+            cost_estimate=pl.CostEstimate(flops=flops, bytes_accessed=x.size * 4, transcendentals=0),
         )(*args)
         return jnp.swapaxes(out, 0, 1).reshape(n, h8, 1, c3)
 

time: 74.9 us -> 73.4 us (0.980)
  Pallas kernels: 72.9 us -> 71.4 us
    pallas_call x1, Pallas kernels: 72.9 us -> 71.4 us  [local_blocks(): pl.pallas_call(functools.partial(kernel, dims), out_shape=jax.ShapeDtypeS...]
where the time goes in v6:
time: 73.4 us; the launch traced here: 73.3 us
  Pallas kernels  71.4 us (97%)
  local copies, waits for them, and re-layouts  1.82 us (2%)
    pallas_call x1, Pallas kernels, local_blocks(): pl.pallas_call(functools.partial(kernel, dims), out_shape=jax.ShapeDtypeS...  71.4 us
    reshape x1, local copies, waits for them, and re-layouts, local_blocks(): return jnp.swapaxes(out, 0, 1).reshape(n, h8, 1, c3)  1.82 us

profile of v6, /device:TPU:13, one launch (start us, length us, event | category | flops | bytes accessed | tf_op | source)
XLA Modules:
  0.0 73.3 jit_solution(7810586631484341396)
XLA Ops:
  0.0 71.4 %shard_map.154 = bf16[32,16,320]{2,1,0:T(8,128)(2,1)} custom-call(bf16[16,4,128,256]{3,2,1,0:T(8,128)(2,1)} %bitcast.16, bf16[3,192,128]{2,1,0:T(8,128)(2,1)} %bitcast.23, bf16[1152,128]{1,0:T(8,128)(2,1)} %bitcast.21, bf16[64,128]{1,0:T(8,128)(2,1)} %wp1_h.1, bf16[1152,256]{1,0:T(8,128)(2,1)} %bitcast.20, bf16[2304,256]{1,0:T(8,128)(2,1)} %bitcast.19, ...), custom_call_target="tpu_custom_call" | custom-call | flops 5637144576 | bytes 8388608 | tf_op jit(solution)/shard_map/pallas_call | solution.py:736
  71.4 1.8 %copy.17 = bf16[16,32,1,320]{3,1,2,0:T(8,128)(2,1)} copy(bf16[16,32,1,320]{3,0,1,2:T(8,128)(2,1)} %bitcast.15) | data formatting | bytes 655360 | tf_op jit(solution)/shard_map/reshape | solution.py:753

commit v7 on v6

--- a/solution.py
+++ b/solution.py
@@ -15,7 +15,7 @@
 PAIRS = 4
 MAX_PLAN = 5
 BLOCK = 16
-UNROLL = 4
+UNROLL = 8
 OWN, HALO = BOTH = range(2)
 AROUND = (1, 2, 3)
 NEAR = range(-2, 3)
@@ -198,6 +198,8 @@
         proj_at = 12 * c1
         zero_part(w1c, proj_at + (1 - p) * pair, pair, p)
         zero_part(w1c, proj_at + p * pair + c0, c0, p)
+    for copy in x_loads:
+        copy.wait()
     pl.semaphore_wait(barrier, around)
 
     def remote(src, dst, send_sem, recv_sem, to_row, to_col):
@@ -207,9 +209,9 @@
     def x_copy(shift, half):
         lanes = pl.ds(half * hh, hh)
         if shift == 0:
-            src, dst = x_hbm.at[:, 3, pl.ds(c0, c0), lanes], xh.at[half, :, pl.ds(c0, c0)]
+            src, dst = raw.at[PAIRS - 1, :, pl.ds(c0, c0), lanes], xh.at[half, :, pl.ds(c0, c0)]
         else:
-            src, dst = x_hbm.at[:, 0, :, lanes], xh.at[half]
+            src, dst = raw.at[0, :, :, lanes], xh.at[half]
         return remote(src, dst, x_sem.at[half], x_sem.at[2 + half], row, fwd_col)
 
     for shift in SHIFTS:
@@ -314,30 +316,29 @@
     def turn_halo(half):
         slot = jnp.where(is0, 1, PAIRS + 1)
         unit = eye[:hh, :hh]
+        many = min(UNROLL, n // 2)
 
         def turn(i, carry):
-            for j in range(UNROLL):
-                at = 2 * (i * UNROLL + j)
+            for j in range(many):
+                at = 2 * (i * many + j)
                 block = xh[half, pl.ds(at, 2)].reshape(2 * pair, hh)
                 both = lax.dot_general(unit, block, NT, preferred_element_type=F32).astype(BF16)
                 for side in BOTH:
                     turned[at + side, :hh, :pair] = both[:, side * pair:(side + 1) * pair]
             return carry
-        loop(n // 2 // UNROLL, turn)
-
-        def place(i, carry):
+        loop(n // 2 // many, turn)
+
+        def place(i):
             blocks = [turned[:, pl.ds((2 * i + j) * BLOCK, BLOCK), :pair].reshape(n * BLOCK, pair) for j in BOTH]
             moved = dot(mix[...], jnp.concatenate(blocks, axis=1))
             for j in BOTH:
                 first = 1 + half * (h4 // 2) + (2 * i + j) * (BLOCK // 4)
                 xs[slot, pl.ds(first, BLOCK // 4)] = to_rows(moved[:, j * pair:(j + 1) * pair])
-            return carry
-        loop(hh // BLOCK // 2, place)
+        for i in range(hh // BLOCK // 2):
+            place(i)
 
     for copy in w1d_loads + w1c_loads + w2d_loads + w2c_loads + w3d_loads + w3c_loads:
         copy.start()
-    for copy in x_loads:
-        copy.wait()
 
     def flat(value):
         return value.reshape(value.shape[0] * n, value.shape[-1])
@@ -386,6 +387,17 @@
     row_messages("x", "send")
     for copy in w1d_loads:
         copy.wait()
+    def turn_weight(i, carry):
+        for j in range(3):
+            tap = 3 * i + j
+            w3d[tap] = dot_nt(eye[:c2, :c2], w3r[tap]).astype(BF16)
+        return carry
+
+    def turn_weights():
+        for copy in w3d_loads:
+            copy.wait()
+        loop(3, turn_weight)
+
     early = 3 - t_first
 
     def y1_item(item, carry):
@@ -394,6 +406,10 @@
             row_messages("x", "recv")
 
         half = item - 2 * early
+
+        @pl.when((half == 1) & jnp.logical_not(is0))
+        def _():
+            turn_weights()
 
         @pl.when(half >= 0)
         def _():
@@ -453,12 +469,6 @@
 
     extra = -t_first
 
-    def turn_weight(i, carry):
-        for j in range(3):
-            tap = 3 * i + j
-            w3d[tap] = dot_nt(eye[:c2, :c2], w3r[tap]).astype(BF16)
-        return carry
-
     def z1_item(item, carry):
         inner = item - extra
         edge = inner - NCH - extra
@@ -471,11 +481,9 @@
         half = lax.rem(edge, 2)
         far = edge >= 2
 
-        @pl.when(edge == 0)
-        def _():
-            for copy in w3d_loads:
-                copy.wait()
-            loop(3, turn_weight)
+        @pl.when((edge == 0) & is0)
+        def _():
+            turn_weights()
 
         @pl.when((edge >= 0) & (edge < 2))
         def _():

time: 73.4 us -> 73.9 us (level)
  no operation moved by 1% of the time
where the time goes in v7:
time: 73.9 us; the launch traced here: 73.7 us
  Pallas kernels  71.9 us (97%)
  local copies, waits for them, and re-layouts  1.82 us (2%)
    pallas_call x1, Pallas kernels, local_blocks(): pl.pallas_call(functools.partial(kernel, dims), out_shape=jax.ShapeDtypeS...  71.9 us
    reshape x1, local copies, waits for them, and re-layouts, local_blocks(): return jnp.swapaxes(out, 0, 1).reshape(n, h8, 1, c3)  1.82 us

profile of v7, /device:TPU:13, one launch (start us, length us, event | category | flops | bytes accessed | tf_op | source)
XLA Modules:
  0.0 73.7 jit_solution(6369083848193208534)
XLA Ops:
  0.0 71.9 %shard_map.154 = bf16[32,16,320]{2,1,0:T(8,128)(2,1)} custom-call(bf16[16,4,128,256]{3,2,1,0:T(8,128)(2,1)} %bitcast.16, bf16[3,192,128]{2,1,0:T(8,128)(2,1)} %bitcast.23, bf16[1152,128]{1,0:T(8,128)(2,1)} %bitcast.21, bf16[64,128]{1,0:T(8,128)(2,1)} %wp1_h.1, bf16[1152,256]{1,0:T(8,128)(2,1)} %bitcast.20, bf16[2304,256]{1,0:T(8,128)(2,1)} %bitcast.19, ...), custom_call_target="tpu_custom_call" | custom-call | flops 5637144576 | bytes 8388608 | tf_op jit(solution)/shard_map/pallas_call | solution.py:744
  71.9 1.8 %copy.17 = bf16[16,32,1,320]{3,1,2,0:T(8,128)(2,1)} copy(bf16[16,32,1,320]{3,0,1,2:T(8,128)(2,1)} %bitcast.15) | data formatting | bytes 655360 | tf_op jit(solution)/shard_map/reshape | solution.py:761

commit v8 on v7

--- a/solution.py
+++ b/solution.py
@@ -630,51 +630,48 @@
         copy.wait()
 
     ships = (s == 1) & has_bwd
-
-    def ship(c):
-        part = pl.ds(c * ch3, ch3)
-        return remote(zo.at[1, part], out_hbm.at[part], out_sem.at[c], out_sem.at[NCH3 + c], row, bwd_col)
-
-    def ship_recv(c):
-        part = pl.ds(c * ch3, ch3)
-        return remote(zo.at[1, part], out_hbm.at[part], out_sem.at[c], out_sem.at[NCH3 + c], row, fwd_col)
+    z3_parts = ((0, ch3 - 1), (ch3 - 1, ch3 + 1))
+
+    def ship(c, to_col):
+        part = pl.ds(*z3_parts[c])
+        return remote(zo.at[1, part], out_hbm.at[part], out_sem.at[c], out_sem.at[NCH3 + c], row, to_col)
 
     keep = jnp.where(is0, 1, 0)
 
     def put(c):
-        part = pl.ds(c * ch3, ch3)
+        part = pl.ds(*z3_parts[c])
         return pltpu.make_async_copy(zo.at[keep, part], out_hbm.at[part], out_sem.at[2 * NCH3 + c])
 
-    def z3_item(t, c):
-        k = t
-
-        @pl.when((t == t_first) & (c == 0))
+    def z3_col(i, carry):
+        k = t_first + i
+
+        @pl.when(i == 0)
         def _():
             row_messages("y3", "recv")
 
-        @pl.when((t == 0) & (c == 0))
-        def _():
-            for forward, exists in ((False, has_fwd), (True, has_bwd)):
-                @pl.when(exists)
-                def _():
-                    for chunk in range(NCH3):
-                        y_recv(y3, 1, ch3, SEM_Y3, forward, chunk, NCH3).wait_recv()
-
-        for at, size in whole(c):
-            acc = dot_nt(flat(z2[2 * k + 3, pl.ds(at, size), 0]), wp3r[...]) + b3c[...]
-            taps = [flat(y3[k + side, pl.ds(first, size)]) for first in (at - 1, at, at + 1) for side in AROUND]
+        for c, (first, size) in enumerate(z3_parts):
+            @pl.when(k == 0)
+            def _():
+                for forward, exists in ((False, has_fwd), (True, has_bwd)):
+                    @pl.when(exists)
+                    def _():
+                        y_recv(y3, 1, ch3, SEM_Y3, forward, c, NCH3).wait_recv()
+
+            acc = dot_nt(flat(z2[2 * k + 3, pl.ds(1 + first, size), 0]), wp3r[...]) + b3c[...]
+            taps = [flat(y3[k + side, pl.ds(first + down, size)]) for down in range(3) for side in AROUND]
             acc = acc + dot(jnp.concatenate([tap[:, :c2] for tap in taps], axis=1), w3c[...].reshape(k2, c3))
             acc = acc + dot(jnp.concatenate([tap[:, c2:] for tap in taps], axis=1), w3e[...].reshape(9 * (c3 - c2), c3))
-            zo[k + 1, pl.ds(at - 1, size)] = relu(acc).astype(BF16).reshape(size, n, c3)
-
-        @pl.when((t == 0) & ships)
-        def _():
-            ship(c).start()
-
-        @pl.when(((t == 0) & is0) | (t == -1))
-        def _():
-            put(c).start()
-    phase(1, NCH3, z3_item)
+            zo[k + 1, pl.ds(first, size)] = relu(acc).astype(BF16).reshape(size, n, c3)
+
+            @pl.when((k == 0) & ships)
+            def _():
+                ship(c, bwd_col).start()
+
+            @pl.when(((k == 0) & is0) | (k == -1))
+            def _():
+                put(c).start()
+        return carry
+    loop(1 + extra, z3_col)
 
     for shift in SHIFTS:
         @pl.when(has_fwd & (s == shift))
@@ -697,7 +694,7 @@
         return carry
     loop(NCH, drain)
 
-    def drain3(c, carry):
+    def drain3(c):
         @pl.when(has_fwd)
         def _():
             y_copy(y3, 1, ch3, SEM_Y3, True, c, NCH3).wait_send()
@@ -708,17 +705,17 @@
 
         @pl.when(ships)
         def _():
-            ship(c).wait_send()
+            ship(c, bwd_col).wait_send()
 
         @pl.when((s == 1) & has_fwd)
         def _():
-            ship_recv(c).wait_recv()
+            ship(c, fwd_col).wait_recv()
 
         @pl.when(is0 | first_extra)
         def _():
             put(c).wait()
-        return carry
-    loop(NCH3, drain3)
+    for c in range(NCH3):
+        drain3(c)
     for name in ROW_SEM:
         row_messages(name, "sent")
 

time: 73.9 us -> 72 us (0.974)
  Pallas kernels: 71.9 us -> 70 us
    pallas_call x1, Pallas kernels: 71.9 us -> 70 us  [local_blocks(): pl.pallas_call(functools.partial(kernel, dims), out_shape=jax.ShapeDtypeS...]
where the time goes in v8:
time: 72 us; the launch traced here: 71.9 us
  Pallas kernels  70 us (97%)
  local copies, waits for them, and re-layouts  1.82 us (3%)
    pallas_call x1, Pallas kernels, local_blocks(): pl.pallas_call(functools.partial(kernel, dims), out_shape=jax.ShapeDtypeS...  70 us
    reshape x1, local copies, waits for them, and re-layouts, local_blocks(): return jnp.swapaxes(out, 0, 1).reshape(n, h8, 1, c3)  1.82 us

profile of v8, /device:TPU:13, one launch (start us, length us, event | category | flops | bytes accessed | tf_op | source)
XLA Modules:
  0.0 71.9 jit_solution(10843815298651392476)
XLA Ops:
  0.0 70.0 %shard_map.154 = bf16[32,16,320]{2,1,0:T(8,128)(2,1)} custom-call(bf16[16,4,128,256]{3,2,1,0:T(8,128)(2,1)} %bitcast.16, bf16[3,192,128]{2,1,0:T(8,128)(2,1)} %bitcast.23, bf16[1152,128]{1,0:T(8,128)(2,1)} %bitcast.21, bf16[64,128]{1,0:T(8,128)(2,1)} %wp1_h.1, bf16[1152,256]{1,0:T(8,128)(2,1)} %bitcast.20, bf16[2304,256]{1,0:T(8,128)(2,1)} %bitcast.19, ...), custom_call_target="tpu_custom_call" | custom-call | flops 5637144576 | bytes 8388608 | tf_op jit(solution)/shard_map/pallas_call | solution.py:741
  70.0 1.8 %copy.17 = bf16[16,32,1,320]{3,1,2,0:T(8,128)(2,1)} copy(bf16[16,32,1,320]{3,0,1,2:T(8,128)(2,1)} %bitcast.15) | data formatting | bytes 655360 | tf_op jit(solution)/shard_map/reshape | solution.py:758

commit v9 on v8

--- a/solution.py
+++ b/solution.py
@@ -407,10 +407,6 @@
 
         half = item - 2 * early
 
-        @pl.when((half == 1) & jnp.logical_not(is0))
-        def _():
-            turn_weights()
-
         @pl.when(half >= 0)
         def _():
             for shift in SHIFTS:
@@ -569,6 +565,10 @@
         acc = dot(jnp.concatenate(taps, axis=1), w2c[...])
         val = relu(acc + b2c[...]).astype(BF16).reshape(ch // 2, 2, n, c2)
         z2[k + 3 - s, pl.ds(1 + c * (ch // 2), ch // 2)] = val
+
+    @pl.when(jnp.logical_not(is0))
+    def _():
+        turn_weights()
 
     row_messages("y2", "recv")
 

time: 72 us -> 72 us (level)
  no operation moved by 1% of the time
where the time goes in v9:
time: 72 us; the launch traced here: 71.8 us
  Pallas kernels  70 us (97%)
  local copies, waits for them, and re-layouts  1.82 us (3%)
    pallas_call x1, Pallas kernels, local_blocks(): pl.pallas_call(functools.partial(kernel, dims), out_shape=jax.ShapeDtypeS...  70 us
    reshape x1, local copies, waits for them, and re-layouts, local_blocks(): return jnp.swapaxes(out, 0, 1).reshape(n, h8, 1, c3)  1.82 us

profile of v9, /device:TPU:13, one launch (start us, length us, event | category | flops | bytes accessed | tf_op | source)
XLA Modules:
  0.0 71.8 jit_solution(14965539019896533925)
XLA Ops:
  0.0 70.0 %shard_map.154 = bf16[32,16,320]{2,1,0:T(8,128)(2,1)} custom-call(bf16[16,4,128,256]{3,2,1,0:T(8,128)(2,1)} %bitcast.16, bf16[3,192,128]{2,1,0:T(8,128)(2,1)} %bitcast.23, bf16[1152,128]{1,0:T(8,128)(2,1)} %bitcast.21, bf16[64,128]{1,0:T(8,128)(2,1)} %wp1_h.1, bf16[1152,256]{1,0:T(8,128)(2,1)} %bitcast.20, bf16[2304,256]{1,0:T(8,128)(2,1)} %bitcast.19, ...), custom_call_target="tpu_custom_call" | custom-call | flops 5637144576 | bytes 8388608 | tf_op jit(solution)/shard_map/pallas_call | solution.py:741
  70.0 1.8 %copy.17 = bf16[16,32,1,320]{3,1,2,0:T(8,128)(2,1)} copy(bf16[16,32,1,320]{3,0,1,2:T(8,128)(2,1)} %bitcast.15) | data formatting | bytes 655360 | tf_op jit(solution)/shard_map/reshape | solution.py:758

commit v10 on v9

--- a/solution.py
+++ b/solution.py
@@ -249,6 +249,9 @@
         return remote(ref.at[dst_slot, part], ref.at[dst_slot, part], col_send.at[sem], col_recv.at[sem], row, bwd_col)
 
     SEM_Y1, SEM_Z1, SEM_Y2, SEM_Z2, SEM_Y3 = (i * 2 * NCH for i in range(5))
+    y1_whole = (y1, PAIRS, h4, SEM_Y1, True, 0, 1)
+    z1_half = (z1, PAIRS, 2 * ch, SEM_Z1)
+    z2_half = (z2, 2, ch, SEM_Z2)
 
     def row_messages(name, act, ways=None):
         kind, width, sem0 = ROW_SEM[name]
@@ -427,9 +430,9 @@
         send_edges("y1", half, 2)
 
         for t, c in jobs:
-            @pl.when((t == 0) & has_fwd)
+            @pl.when((t == 0) & (c == 0) & has_fwd)
             def _():
-                y_copy(y1, PAIRS, ch, SEM_Y1, True, c, NCH).start()
+                y_copy(*y1_whole).start()
 
             @pl.when((t == 3) & has_bwd)
             def _():
@@ -485,9 +488,9 @@
         def _():
             wait_halo(y1, PAIRS, ch, SEM_Y1, False, half, NCH)
 
-        @pl.when(far)
-        def _():
-            wait_halo(y1, PAIRS, ch, SEM_Y1, True, half, NCH)
+        @pl.when((edge == 2) & has_bwd)
+        def _():
+            y_recv(*y1_whole).wait_recv()
 
         mid = jnp.where(inner < 2, inner + 1, jnp.where(inner == 2, 0, inner))
         edge_col = jnp.where(far, 3, 0)
@@ -498,8 +501,7 @@
 
         @pl.when((edge >= 0) & (edge < 2) & has_fwd)
         def _():
-            for j in BOTH:
-                z_copy(z1, PAIRS, ch, SEM_Z1, 2 * half + j).start()
+            z_copy(*z1_half, half).start()
         return carry
     loop(2 * (NCH + extra), z1_item)
     row_messages("z1", "send")
@@ -537,9 +539,9 @@
     loop(2 + 2 * extra, y2_inner)
 
     def y2_edge(c, carry):
-        @pl.when(has_bwd)
-        def _():
-            z_recv(z1, PAIRS, ch, SEM_Z1, c).wait_recv()
+        @pl.when(has_bwd & (lax.rem(c, 2) == 0))
+        def _():
+            z_recv(*z1_half, lax.div(c, 2)).wait_recv()
 
         for at, size in parts(1 + c * ch, ch):
             y2_job(jnp.int32(1), at, size)
@@ -590,8 +592,7 @@
 
         @pl.when(near & has_fwd)
         def _():
-            for j in BOTH:
-                z_copy(z2, 2, ch // 2, SEM_Z2, 2 * half + j).start()
+            z_copy(*z2_half, half).start()
         return carry
     loop(NCH + 2 * extra, z2_item)
     row_messages("z2", "send")
@@ -605,8 +606,7 @@
 
         @pl.when((t == 0) & has_bwd)
         def _():
-            for j in range(NCH // NCH3):
-                z_recv(z2, 2, ch // 2, SEM_Z2, c * (NCH // NCH3) + j).wait_recv()
+            z_recv(*z2_half, c).wait_recv()
 
         for at, size in whole(c):
             taps = [flat(z2[2 * k + 2 + side, pl.ds(first, size), sub]) for first, sub in rows_down(at) for side in range(3)]
@@ -682,10 +682,7 @@
     def drain(c, carry):
         @pl.when(has_fwd)
         def _():
-            y_copy(y1, PAIRS, ch, SEM_Y1, True, c, NCH).wait_send()
-            z_copy(z1, PAIRS, ch, SEM_Z1, c).wait_send()
             y_copy(y2, 2, ch, SEM_Y2, True, c, NCH).wait_send()
-            z_copy(z2, 2, ch // 2, SEM_Z2, c).wait_send()
 
         @pl.when(has_bwd)
         def _():
@@ -693,6 +690,13 @@
             y_copy(y2, 2, ch, SEM_Y2, False, c, NCH).wait_send()
         return carry
     loop(NCH, drain)
+
+    @pl.when(has_fwd)
+    def _():
+        y_copy(*y1_whole).wait_send()
+        for half in BOTH:
+            z_copy(*z1_half, half).wait_send()
+            z_copy(*z2_half, half).wait_send()
 
     def drain3(c):
         @pl.when(has_fwd)

time: 72 us -> 72 us (level)
  no operation moved by 1% of the time
where the time goes in v10:
time: 72 us; the launch traced here: 71.9 us
  Pallas kernels  70.1 us (97%)
  local copies, waits for them, and re-layouts  1.82 us (3%)
    pallas_call x1, Pallas kernels, local_blocks(): pl.pallas_call(functools.partial(kernel, dims), out_shape=jax.ShapeDtypeS...  70.1 us
    reshape x1, local copies, waits for them, and re-layouts, local_blocks(): return jnp.swapaxes(out, 0, 1).reshape(n, h8, 1, c3)  1.82 us

profile of v10, /device:TPU:13, one launch (start us, length us, event | category | flops | bytes accessed | tf_op | source)
XLA Modules:
  0.0 71.9 jit_solution(12955486234716577032)
XLA Ops:
  0.0 70.1 %shard_map.154 = bf16[32,16,320]{2,1,0:T(8,128)(2,1)} custom-call(bf16[16,4,128,256]{3,2,1,0:T(8,128)(2,1)} %bitcast.16, bf16[3,192,128]{2,1,0:T(8,128)(2,1)} %bitcast.23, bf16[1152,128]{1,0:T(8,128)(2,1)} %bitcast.21, bf16[64,128]{1,0:T(8,128)(2,1)} %wp1_h.1, bf16[1152,256]{1,0:T(8,128)(2,1)} %bitcast.20, bf16[2304,256]{1,0:T(8,128)(2,1)} %bitcast.19, ...), custom_call_target="tpu_custom_call" | custom-call | flops 5637144576 | bytes 8388608 | tf_op jit(solution)/shard_map/pallas_call | solution.py:745
  70.1 1.8 %copy.17 = bf16[16,32,1,320]{3,1,2,0:T(8,128)(2,1)} copy(bf16[16,32,1,320]{3,0,1,2:T(8,128)(2,1)} %bitcast.15) | data formatting | bytes 655360 | tf_op jit(solution)/shard_map/reshape | solution.py:762

commit v11 on v9

--- a/solution.py
+++ b/solution.py
@@ -630,17 +630,19 @@
         copy.wait()
 
     ships = (s == 1) & has_bwd
-    z3_parts = ((0, ch3 - 1), (ch3 - 1, ch3 + 1))
+    low, mid = ch3 - 1, ch3 // 2
+    z3_parts = ((0, low), (low, mid), (low + mid, mid + 1))
+    n_parts = len(z3_parts)
 
     def ship(c, to_col):
         part = pl.ds(*z3_parts[c])
-        return remote(zo.at[1, part], out_hbm.at[part], out_sem.at[c], out_sem.at[NCH3 + c], row, to_col)
+        return remote(zo.at[1, part], out_hbm.at[part], out_sem.at[c], out_sem.at[n_parts + c], row, to_col)
 
     keep = jnp.where(is0, 1, 0)
 
     def put(c):
         part = pl.ds(*z3_parts[c])
-        return pltpu.make_async_copy(zo.at[keep, part], out_hbm.at[part], out_sem.at[2 * NCH3 + c])
+        return pltpu.make_async_copy(zo.at[keep, part], out_hbm.at[part], out_sem.at[2 * n_parts + c])
 
     def z3_col(i, carry):
         k = t_first + i
@@ -650,12 +652,13 @@
             row_messages("y3", "recv")
 
         for c, (first, size) in enumerate(z3_parts):
-            @pl.when(k == 0)
-            def _():
-                for forward, exists in ((False, has_fwd), (True, has_bwd)):
-                    @pl.when(exists)
-                    def _():
-                        y_recv(y3, 1, ch3, SEM_Y3, forward, c, NCH3).wait_recv()
+            if c < NCH3:
+                @pl.when(k == 0)
+                def _():
+                    for forward, exists in ((False, has_fwd), (True, has_bwd)):
+                        @pl.when(exists)
+                        def _():
+                            y_recv(y3, 1, ch3, SEM_Y3, forward, c, NCH3).wait_recv()
 
             acc = dot_nt(flat(z2[2 * k + 3, pl.ds(1 + first, size), 0]), wp3r[...]) + b3c[...]
             taps = [flat(y3[k + side, pl.ds(first + down, size)]) for down in range(3) for side in AROUND]
@@ -702,20 +705,23 @@
         @pl.when(has_bwd)
         def _():
             y_copy(y3, 1, ch3, SEM_Y3, False, c, NCH3).wait_send()
-
-        @pl.when(ships)
-        def _():
-            ship(c, bwd_col).wait_send()
-
-        @pl.when((s == 1) & has_fwd)
-        def _():
-            ship(c, fwd_col).wait_recv()
-
-        @pl.when(is0 | first_extra)
-        def _():
-            put(c).wait()
     for c in range(NCH3):
         drain3(c)
+
+    def drain_out(c):
+        @pl.when(ships)
+        def _():
+            ship(c, bwd_col).wait_send()
+
+        @pl.when((s == 1) & has_fwd)
+        def _():
+            ship(c, fwd_col).wait_recv()
+
+        @pl.when(is0 | first_extra)
+        def _():
+            put(c).wait()
+    for c in range(n_parts):
+        drain_out(c)
     for name in ROW_SEM:
         row_messages(name, "sent")
 
@@ -751,7 +757,7 @@
                     (10 * pair, 2 * c1), (12 * c1 + 2 * pair, 2 * c1), (9 * c1, c2), (9 * c2 + c1, c2),
                     (9, c3, c2), (9, c2, c3), (9, c2, c3), (9, c3 - c2, c3), (c3, c2))
             ] + [vm((1, width), F32) for width in (c1, c1, c2, c2, c3, c3)] + [
-                dma((count,)) for count in (32, 4, 10 * NCH, 10 * NCH, 12 * MAX_PLAN, 12 * MAX_PLAN, 3 * NCH3)],
+                dma((count,)) for count in (32, 4, 10 * NCH, 10 * NCH, 12 * MAX_PLAN, 12 * MAX_PLAN, 5 * NCH3)],
             compiler_params=pltpu.CompilerParams(collective_id=0, has_side_effects=True, vmem_limit_bytes=63 << 20),
             cost_estimate=pl.CostEstimate(flops=flops, bytes_accessed=x.size * 4, transcendentals=0),
         )(*args)

time: 72 us -> 72 us (level)
  no operation moved by 1% of the time
where the time goes in v11:
time: 72 us; the launch traced here: 71.8 us
  Pallas kernels  70 us (97%)
  local copies, waits for them, and re-layouts  1.82 us (3%)
    pallas_call x1, Pallas kernels, local_blocks(): pl.pallas_call(functools.partial(kernel, dims), out_shape=jax.ShapeDtypeS...  70 us
    reshape x1, local copies, waits for them, and re-layouts, local_blocks(): return jnp.swapaxes(out, 0, 1).reshape(n, h8, 1, c3)  1.82 us

profile of v11, /device:TPU:13, one launch (start us, length us, event | category | flops | bytes accessed | tf_op | source)
XLA Modules:
  0.0 71.8 jit_solution(12059955152522405159)
XLA Ops:
  0.0 70.0 %shard_map.154 = bf16[32,16,320]{2,1,0:T(8,128)(2,1)} custom-call(bf16[16,4,128,256]{3,2,1,0:T(8,128)(2,1)} %bitcast.16, bf16[3,192,128]{2,1,0:T(8,128)(2,1)} %bitcast.23, bf16[1152,128]{1,0:T(8,128)(2,1)} %bitcast.21, bf16[64,128]{1,0:T(8,128)(2,1)} %wp1_h.1, bf16[1152,256]{1,0:T(8,128)(2,1)} %bitcast.20, bf16[2304,256]{1,0:T(8,128)(2,1)} %bitcast.19, ...), custom_call_target="tpu_custom_call" | custom-call | flops 5637144576 | bytes 8388608 | tf_op jit(solution)/shard_map/pallas_call | solution.py:747
  70.0 1.8 %copy.17 = bf16[16,32,1,320]{3,1,2,0:T(8,128)(2,1)} copy(bf16[16,32,1,320]{3,0,1,2:T(8,128)(2,1)} %bitcast.15) | data formatting | bytes 655360 | tf_op jit(solution)/shard_map/reshape | solution.py:764

commit v12 on v11

--- a/solution.py
+++ b/solution.py
@@ -645,7 +645,7 @@
         return pltpu.make_async_copy(zo.at[keep, part], out_hbm.at[part], out_sem.at[2 * n_parts + c])
 
     def z3_col(i, carry):
-        k = t_first + i
+        k = -i
 
         @pl.when(i == 0)
         def _():

time: 72 us -> 72.1 us (level)
  no operation moved by 1% of the time
where the time goes in v12:
time: 72.1 us; the launch traced here: 71.4 us
  Pallas kernels  69.6 us (97%)
  local copies, waits for them, and re-layouts  1.82 us (3%)
    pallas_call x1, Pallas kernels, local_blocks(): pl.pallas_call(functools.partial(kernel, dims), out_shape=jax.ShapeDtypeS...  69.6 us
    reshape x1, local copies, waits for them, and re-layouts, local_blocks(): return jnp.swapaxes(out, 0, 1).reshape(n, h8, 1, c3)  1.82 us

profile of v12, /device:TPU:13, one launch (start us, length us, event | category | flops | bytes accessed | tf_op | source)
XLA Modules:
  0.0 71.4 jit_solution(9826628140129664240)
XLA Ops:
  0.0 69.6 %shard_map.154 = bf16[32,16,320]{2,1,0:T(8,128)(2,1)} custom-call(bf16[16,4,128,256]{3,2,1,0:T(8,128)(2,1)} %bitcast.16, bf16[3,192,128]{2,1,0:T(8,128)(2,1)} %bitcast.23, bf16[1152,128]{1,0:T(8,128)(2,1)} %bitcast.21, bf16[64,128]{1,0:T(8,128)(2,1)} %wp1_h.1, bf16[1152,256]{1,0:T(8,128)(2,1)} %bitcast.20, bf16[2304,256]{1,0:T(8,128)(2,1)} %bitcast.19, ...), custom_call_target="tpu_custom_call" | custom-call | flops 5637144576 | bytes 8388608 | tf_op jit(solution)/shard_map/pallas_call | solution.py:747
  69.6 1.8 %copy.17 = bf16[16,32,1,320]{3,1,2,0:T(8,128)(2,1)} copy(bf16[16,32,1,320]{3,0,1,2:T(8,128)(2,1)} %bitcast.15) | data formatting | bytes 655360 | tf_op jit(solution)/shard_map/reshape | solution.py:764
